TPU v7x, 32 devices: a whole 2x2x4 slice. The times are simulated.
32 devices in a mesh: my: 8 (over z, y), mx: 4 (over x, core).
Axes of the slice: x: 2, y: 2, z: 4, core: 2. Of those that a mesh axis runs over, the one named last changes fastest.
Arguments:
- x_in: bfloat16 [192, 5120], P(None, 'mx')
- seq_lens: int32 [192], P('mx')
- gain_attn: bfloat16 [5120], P('mx')
- gain_mlp: bfloat16 [5120], P('mx')
- w_q: bfloat16 [5120, 5120], P('mx', 'my')
- b_q: bfloat16 [5120], P('my')
- w_k: bfloat16 [5120, 1024], P('mx', 'my')
- b_k: bfloat16 [1024], P('my')
- w_v: bfloat16 [5120, 1024], P('mx', 'my')
- b_v: bfloat16 [1024], P('my')
- w_o: bfloat16 [5120, 5120], P('my', 'mx')
- w_gate: bfloat16 [5120, 27392], P('mx', 'my')
- w_up: bfloat16 [5120, 27392], P('mx', 'my')
- w_down: bfloat16 [27392, 5120], P('my', 'mx')
- k_cache: bfloat16 [192, 384, 8, 128], P('mx', None, 'my')
- v_cache: bfloat16 [192, 384, 8, 128], P('mx', None, 'my')
Outputs:
- output 1: bfloat16 [192, 5120], P(None, 'mx')
- output 2: bfloat16 [192, 384, 8, 128], P('mx', None, 'my')
- output 3: bfloat16 [192, 384, 8, 128], P('mx', None, 'my')
All inputs are finite; a program needn't handle non-finite values.
Results may differ from a plain program's by a relative error of at most 0.0177699.
Values are sent between devices in bfloat16 or wider.
A program may use at most 1 GiB of HBM per device.

v0:
```python
import jax
import jax.numpy as jnp
from jax import lax
from jax.sharding import PartitionSpec as P

HEAD = 128
NORM_EPS = 1e-6
ROPE_THETA = 1000000.0


def apply_rotary(vectors, positions):
    half_dim = HEAD // 2
    inv_freq = ROPE_THETA ** (-2.0 * jnp.arange(half_dim, dtype=jnp.float32) / HEAD)
    angles = positions.astype(jnp.float32)[:, None, None] * inv_freq
    cos_tab = jnp.cos(angles)
    sin_tab = jnp.sin(angles)
    lower_half = vectors[..., :half_dim]
    upper_half = vectors[..., half_dim:]
    return jnp.concatenate([lower_half * cos_tab - upper_half * sin_tab, upper_half * cos_tab + lower_half * sin_tab], axis=-1)


def attend_local(q_rot, k_cache_out, v_cache_out, seq_lens):
    row_count, seq_len, kv_heads, _ = k_cache_out.shape
    q_heads = q_rot.shape[1]
    q_grouped = q_rot.reshape(row_count, kv_heads, q_heads // kv_heads, HEAD)
    scores = jnp.einsum("bkgd,bskd->bkgs", q_grouped, k_cache_out, preferred_element_type=jnp.float32) * HEAD ** -0.5
    visible = (jnp.arange(seq_len)[None, :] <= seq_lens[:, None])[:, None, None, :]
    scores = jnp.where(visible, scores, -jnp.inf)
    weights = jnp.exp(scores - jnp.max(scores, axis=-1, keepdims=True))
    weight_sum = jnp.sum(weights, axis=-1, keepdims=True)
    weighted = jnp.einsum("bkgs,bskd->bkgd", weights.astype(jnp.bfloat16), v_cache_out, preferred_element_type=jnp.float32)
    return (weighted / weight_sum).astype(jnp.bfloat16).reshape(row_count, q_heads * HEAD)


def solution(mesh):
    mx_size = mesh.shape["mx"]
    act_spec = P(None, "mx")
    cache_spec = P("mx", None, "my", None)
    in_specs = (act_spec, P("mx"), P("mx"), P("mx"), P("mx", "my"), P("my"), P("mx", "my"), P("my"), P("mx", "my"), P("my"), P("my", "mx"), P("mx", "my"), P("mx", "my"), P("my", "mx"), cache_spec, cache_spec)
    out_specs = (act_spec, cache_spec, cache_spec)

    def local_layer(x_in, seq_lens, gain_attn, gain_mlp, w_q, b_q, w_k, b_k, w_v, b_v, w_o, w_gate, w_up, w_down, k_cache, v_cache):
        hidden = x_in.shape[1] * mx_size
        x_f32 = x_in.astype(jnp.float32)
        attn_sq = lax.psum(jnp.sum(x_f32 * x_f32, axis=1, keepdims=True), "mx")
        normed = (x_f32 * lax.rsqrt(attn_sq / hidden + NORM_EPS) * gain_attn.astype(jnp.float32)).astype(jnp.bfloat16)
        q_cols = w_q.shape[1]
        kv_cols = w_k.shape[1]
        partials = jnp.concatenate([
            jnp.dot(normed, w_q, preferred_element_type=jnp.float32).astype(jnp.bfloat16),
            jnp.dot(normed, w_k, preferred_element_type=jnp.float32).astype(jnp.bfloat16),
            jnp.dot(normed, w_v, preferred_element_type=jnp.float32).astype(jnp.bfloat16),
        ], axis=1)
        projected = lax.psum_scatter(partials, "mx", scatter_dimension=0, tiled=True).astype(jnp.float32)
        row_count = projected.shape[0]
        kv_heads = kv_cols // HEAD
        q_vals = projected[:, :q_cols] + b_q.astype(jnp.float32)
        k_vals = projected[:, q_cols:q_cols + kv_cols] + b_k.astype(jnp.float32)
        v_vals = projected[:, q_cols + kv_cols:] + b_v.astype(jnp.float32)
        q_rot = apply_rotary(q_vals.reshape(row_count, q_cols // HEAD, HEAD), seq_lens).astype(jnp.bfloat16)
        k_rot = apply_rotary(k_vals.reshape(row_count, kv_heads, HEAD), seq_lens).astype(jnp.bfloat16)
        v_new = v_vals.reshape(row_count, kv_heads, HEAD).astype(jnp.bfloat16)
        at_slot = (jnp.arange(k_cache.shape[1])[None, :] == seq_lens[:, None])[:, :, None, None]
        k_cache_out = jnp.where(at_slot, k_rot[:, None], k_cache)
        v_cache_out = jnp.where(at_slot, v_new[:, None], v_cache)
        attn_rows = attend_local(q_rot, k_cache_out, v_cache_out, seq_lens)
        attn_all = lax.all_gather(attn_rows, "mx", axis=0, tiled=True)
        attn_proj = lax.psum(jnp.dot(attn_all, w_o, preferred_element_type=jnp.float32).astype(jnp.bfloat16), "my")
        x_mid = (x_f32 + attn_proj.astype(jnp.float32)).astype(jnp.bfloat16)
        mid_f32 = x_mid.astype(jnp.float32)
        mlp_sq = lax.psum(jnp.sum(mid_f32 * mid_f32, axis=1, keepdims=True), "mx")
        normed_mlp = (mid_f32 * lax.rsqrt(mlp_sq / hidden + NORM_EPS) * gain_mlp.astype(jnp.float32)).astype(jnp.bfloat16)
        ff_cols = w_gate.shape[1]
        gate_up = lax.psum(jnp.concatenate([
            jnp.dot(normed_mlp, w_gate, preferred_element_type=jnp.float32).astype(jnp.bfloat16),
            jnp.dot(normed_mlp, w_up, preferred_element_type=jnp.float32).astype(jnp.bfloat16),
        ], axis=1), "mx").astype(jnp.float32)
        hidden_act = (jax.nn.silu(gate_up[:, :ff_cols]) * gate_up[:, ff_cols:]).astype(jnp.bfloat16)
        down_proj = lax.psum(jnp.dot(hidden_act, w_down, preferred_element_type=jnp.float32).astype(jnp.bfloat16), "my")
        x_out = (mid_f32 + down_proj.astype(jnp.float32)).astype(jnp.bfloat16)
        return x_out, k_cache_out, v_cache_out

    return jax.shard_map(local_layer, mesh=mesh, in_specs=in_specs, out_specs=out_specs, check_vma=False)
```

profile of v0, /device:TPU:0, one launch (start us, length us, event | category | flops | bytes accessed | tf_op | source)
XLA Modules:
  0.0 305.7 jit_solution(9058486895152853632)
XLA Ops:
  7.3 1.3 fusion.19
  8.6 8.4 %psum.35 = f32[192,1]{0,1:T(1,128)S(1)} all-reduce(f32[192,1]{0,1:T(1,128)S(1)} %bitcast.41), channel_id=1, replica_groups=mesh['my'=8,'mx'=4] {'mx'}, use_global_device_ids=true, to_apply=%region_1.0 | all-reduce | flops 192 | bytes 1536 | tf_op jit(solution)/shard_map/psum | solution.py:45
  17.0 0.7 convert_element_type.96
  17.7 1.5 convolution_convert_fusion.6
  19.2 1.5 convolution_convert_fusion.5
  20.6 2.2 convolution_convert_fusion.4
  22.8 0.8 pad_maximum_fusion.1
  23.8 0.1 iota_compare_fusion.1
  23.9 0.2 multiply_cosine_fusion.1
  24.0 20.5 %reduce-scatter.2.cloned.1.call-done = bf16[48,896]{1,0:T(8,128)(2,1)} async-done(((bf16[192,896]{1,0:T(8,128)(2,1)}), bf16[48,896]{1,0:T(8,128)(2,1)}) %reduce-scatter.2.cloned.1.call-update) | async-done | bytes 86032 | tf_op jit(solution)/shard_map/reduce_scatter | solution.py:54
  44.6 0.9 convert_element_type.101
  45.5 0.2 fusion.47
  45.8 0.1 subtract_convert_fusion
  45.9 4.9 %broadcast_select_fusion.1 = (bf16[48,384,1,128]{3,1,2,0:T(8,128)(2,1)S(1)}, bf16[48,384,1,128]{3,1,2,0:T(8,128)(2,1)S(1)}) fusion(bf16[48,384,1,128]{3,1,2,0:T(8,128)(2,1)} %param.30, pred[48,384]{1,0:T(8,128)(4,1)S(1)} %get-tuple-element.16, bf16[48,128]{1,0:T(8,128)(2,1)S(1)} %pad_maximum_fusion.2, bf16[48,384,1,128]{3,1,2,0:T(8,128)(2,1)} %param.31, ...), kind=kLoop, calls=%fused_computation.7 | loop fusion | flops 4718592 | bytes 18917376 | tf_op jit(solution)/shard_map/jit(_where)/select_n | solution.py:64
  50.8 1.8 fusion.54
  52.7 0.2 fusion.27
  52.9 1.0 fusion.16
  53.9 0.6 copy-done.3
  54.6 5.7 %all_gather.3 = bf16[192,640]{1,0:T(8,128)(2,1)S(1)} all-gather(bf16[48,640]{1,0:T(8,128)(2,1)S(1)} %bitcast.39), channel_id=1, replica_groups=mesh['my'=8,'mx'=4] {'mx'}, dimensions={0}, use_global_device_ids=true | all-gather | bytes 307200 | tf_op jit(solution)/shard_map/all_gather | solution.py:67
  60.3 1.3 convolution_convert_fusion.3
  61.7 72.3 %all-reduce.4.cloned.1.call-done = bf16[192,1280]{1,0:T(8,128)(2,1)} async-done(((bf16[192,1280]{1,0:T(8,128)(2,1)}), bf16[192,1280]{1,0:T(8,128)(2,1)}) %all-reduce.4.cloned.1.call-update) | async-done | bytes 491536 | tf_op jit(solution)/shard_map/psum | solution.py:68
  134.1 1.3 fusion.23
  135.4 5.7 %psum.37 = f32[192,1]{0,1:T(1,128)S(1)} all-reduce(f32[192,1]{0,1:T(1,128)S(1)} %bitcast.40), channel_id=1, replica_groups=mesh['my'=8,'mx'=4] {'mx'}, use_global_device_ids=true, to_apply=%region_7.8 | all-reduce | flops 192 | bytes 1536 | tf_op jit(solution)/shard_map/psum | solution.py:71
  141.0 6.5 %convolution_convert_fusion = bf16[192,3424]{1,0:T(8,128)(2,1)S(1)} fusion(bf16[1280,3424]{0,1:T(8,128)(2,1)} %param.28, bf16[192,1280]{1,0:T(8,128)(2,1)S(1)} %get-tuple-element.4, f32[1280]{0:T(1024)S(1)} %convert_element_type.113, f32[192]{0:T(256)S(1)} %bitcast.45), kind=kOutput, calls=%fused_computation | convolution fusion | flops 1684604928 | bytes 10577664 | tf_op jit(solution)/shard_map/dot_general | solution.py:76
  147.6 6.5 %convolution_convert_fusion.1 = bf16[192,3424]{1,0:T(8,128)(2,1)S(1)} fusion(bf16[1280,3424]{0,1:T(8,128)(2,1)} %param.27, bf16[192,1280]{1,0:T(8,128)(2,1)S(1)} %get-tuple-element.4, f32[1280]{0:T(1024)S(1)} %convert_element_type.113, f32[192]{0:T(256)S(1)} %bitcast.46), kind=kOutput, calls=%fused_computation.1 | convolution fusion | flops 1684604928 | bytes 10577664 | tf_op jit(solution)/shard_map/dot_general | solution.py:75
  154.1 2.1 pad_maximum_fusion
  156.2 0.2 all-reduce.8.cloned.1.call-start
  156.5 59.5 %all-reduce.6.cloned.1.call-done = bf16[192,6848]{1,0:T(8,128)(2,1)} async-done(((bf16[192,6848]{1,0:T(8,128)(2,1)}), bf16[192,6848]{1,0:T(8,128)(2,1)}) %all-reduce.6.cloned.1.call-update) | async-done | bytes 2629648 | tf_op jit(solution)/shard_map/psum | solution.py:74
  215.9 2.1 convert_element_type.117
  218.0 6.8 %convolution_convert_fusion.2 = bf16[192,1280]{1,0:T(8,128)(2,1)} fusion(bf16[3424,1280]{1,0:T(8,128)(2,1)} %param.29, f32[192,6848]{1,0:T(8,128)S(1)} %convert_element_type.117), kind=kOutput, calls=%fused_computation.11 | convolution fusion | flops 1687154688 | bytes 14516224 | tf_op jit(solution)/shard_map/dot_general | solution.py:79
  224.8 72.4 %all-reduce.8.cloned.1.call-done = bf16[192,1280]{1,0:T(8,128)(2,1)} async-done(((bf16[192,1280]{1,0:T(8,128)(2,1)}), bf16[192,1280]{1,0:T(8,128)(2,1)}) %all-reduce.8.cloned.1.call-update) | async-done | bytes 491536 | tf_op jit(solution)/shard_map/psum | solution.py:79
  297.3 1.9 fusion.26
  (39 shorter events, 0.4 us)
Async XLA Ops:
  7.2 53.1 %copy-start = (bf16[640,1280]{1,0:T(8,128)(2,1)S(1)}, bf16[640,1280]{1,0:T(8,128)(2,1)}, u32[]{:S(2)}) copy-start(bf16[640,1280]{1,0:T(8,128)(2,1)} %param.26) | copy-start | bytes 4915204
  7.2 16.5 %copy-start.7 = (s32[48]{0:T(128)S(1)}, s32[48]{0:T(128)}, u32[]{:S(2)}) copy-start(s32[48]{0:T(128)} %param.17) | copy-start | bytes 580
  7.2 16.5 %copy-start.8 = (bf16[128]{0:T(256)(128)(2,1)S(1)}, bf16[128]{0:T(256)(128)(2,1)}, u32[]{:S(2)}) copy-start(bf16[128]{0:T(256)(128)(2,1)} %param.23) | copy-start | bytes 772
  7.2 16.5 %copy-start.9 = (bf16[128]{0:T(256)(128)(2,1)S(1)}, bf16[128]{0:T(256)(128)(2,1)}, u32[]{:S(2)}) copy-start(bf16[128]{0:T(256)(128)(2,1)} %param.25) | copy-start | bytes 772
  7.2 16.5 %copy-start.6 = (bf16[640]{0:T(1024)(128)(2,1)S(1)}, bf16[640]{0:T(1024)(128)(2,1)}, u32[]{:S(2)}) copy-start(bf16[640]{0:T(1024)(128)(2,1)} %param.21) | copy-start | bytes 3844
  7.2 37.3 %reduce-scatter.2.cloned.1.call-start = ((), (), s32[]{:S(2)}) async-start(), calls=%async_computation.1 | async-start | bytes 430080 | tf_op jit(solution)/shard_map/reduce_scatter | solution.py:54
  23.6 110.4 %all-reduce.4.cloned.1.call-start = ((), (), s32[]{:S(2)}) async-start(), calls=%async_computation.2 | async-start | bytes 983040 | tf_op jit(solution)/shard_map/psum | solution.py:68
  50.8 3.1 %copy-start.2 = (bf16[48,384,1,128]{3,1,2,0:T(8,128)(2,1)}, bf16[48,384,1,128]{3,1,2,0:T(8,128)(2,1)S(1)}, u32[]{:S(2)}) copy-start(bf16[48,384,1,128]{3,1,2,0:T(8,128)(2,1)S(1)} %get-tuple-element.11) | copy-start | bytes 14155780
  50.8 3.7 %copy-start.3 = (bf16[48,384,1,128]{3,1,2,0:T(8,128)(2,1)}, bf16[48,384,1,128]{3,1,2,0:T(8,128)(2,1)S(1)}, u32[]{:S(2)}) copy-start(bf16[48,384,1,128]{3,1,2,0:T(8,128)(2,1)S(1)} %get-tuple-element.12) | copy-start | bytes 14155780
  52.7 9.0 %copy-start.5 = (bf16[1280]{0:T(1024)(128)(2,1)S(1)}, bf16[1280]{0:T(1024)(128)(2,1)}, u32[]{:S(2)}) copy-start(bf16[1280]{0:T(1024)(128)(2,1)} %param.19) | copy-start | bytes 7684
  52.7 81.4 %copy-start.4 = (bf16[192,1280]{1,0:T(8,128)(2,1)S(1)}, bf16[192,1280]{1,0:T(8,128)(2,1)}, u32[]{:S(2)}) copy-start(bf16[192,1280]{1,0:T(8,128)(2,1)} %param.16) | copy-start | bytes 1474564
  61.7 154.2 %all-reduce.6.cloned.1.call-start = ((), (), s32[]{:S(2)}) async-start(), calls=%async_computation.3 | async-start | bytes 5308416 | tf_op jit(solution)/shard_map/psum | solution.py:74
  156.2 141.0 %all-reduce.8.cloned.1.call-start = ((), (), s32[]{:S(2)}) async-start(), calls=%async_computation.4 | async-start | bytes 983040 | tf_op jit(solution)/shard_map/psum | solution.py:79
  218.0 81.2 %copy-start.1 = (bf16[640,1280]{1,0:T(8,128)(2,1)S(1)}, bf16[640,1280]{1,0:T(8,128)(2,1)}, u32[]{:S(2)}) copy-start(bf16[640,1280]{1,0:T(8,128)(2,1)} %param.26) | copy-start | bytes 4915204
Sparse Core Ops, SparseCore 0:
  23.7 20.7 reduce-scatter.1
  61.8 72.2 all-reduce.3
  156.3 59.5 all-reduce.5
  224.9 72.2 all-reduce.7
where the time goes:
time: 306 us
  waiting for transfers between devices  225 us (74%)
  matrix products  29.1 us (10%)
  blocking collectives  19.8 us (6%)
  other arithmetic  16.9 us (6%)
  between operations  14 us (5%)
    psum x1, waiting for transfers between devices, local_layer(): lax.psum(jnp.dot(hidden_act, w_down, preferred_element_type=jnp.float32)....  72.4 us
    psum x1, waiting for transfers between devices, local_layer(): lax.psum(jnp.dot(attn_all, w_o, preferred_element_type=jnp.float32).astyp...  72.3 us
    psum x1, waiting for transfers between devices, local_layer(): lax.psum(jnp.concatenate([jnp.dot(normed_mlp, w_gate, preferred_element_t...  59.5 us
    reduce_scatter x1, waiting for transfers between devices, local_layer(): lax.psum_scatter(partials, 'mx', scatter_dimension=0, tiled=True)  20.5 us
    psum x1, blocking collectives, local_layer(): attn_sq = lax.psum(jnp.sum(x_f32 * x_f32, axis=1, keepdims=True), 'mx')  8.4 us
    dot_general x1, matrix products, local_layer(): jnp.dot(hidden_act, w_down, preferred_element_type=jnp.float32)  6.78 us
    dot_general x1, matrix products, local_layer(): jnp.dot(normed_mlp, w_up, preferred_element_type=jnp.float32)  6.54 us
    dot_general x1, matrix products, local_layer(): jnp.dot(normed_mlp, w_gate, preferred_element_type=jnp.float32)  6.54 us
  transfers between devices with their start and end apart: 4, of which 4 were waited for; matrix products, arithmetic and copies ran while one was open for 0% of the time, Pallas kernels for 0%

commit v1 on v0

v1 whole, which is shorter than its diff:
```python
import functools

import jax
import jax.numpy as jnp
from jax import lax
from jax.experimental import pallas as pl
from jax.experimental.pallas import tpu as pltpu
from jax.sharding import PartitionSpec as P

HEAD = 128
NORM_EPS = 1e-6
ROPE_THETA = 1000000.0
MESH = pl.DeviceIdType.MESH
CHUNK = 512
ROWS = 64
LAG_B, LAG_C, LAG_D, LAG_E = 1, 4, 7, 8
VMEM_LIMIT = 66 * 1024 * 1000


def rcopy(src, dst, send_sem, recv_sem, dev):
    return pltpu.make_async_remote_copy(src_ref=src, dst_ref=dst, send_sem=send_sem, recv_sem=recv_sem, device_id=dev, device_id_type=MESH)


def lane_ids():
    return lax.broadcasted_iota(jnp.int32, (8, 128), 1)


def pack_column(blocks):
    tile = jnp.zeros((8, 128), jnp.float32)
    lanes = lane_ids()
    for k, block in enumerate(blocks):
        tile = jnp.where(lanes == k, block, tile)
    return tile


def unpack_column(tile, k):
    return jnp.sum(jnp.where(lane_ids() == k, tile, 0.0), axis=1, keepdims=True)


def qkv_kernel(hidden, x_hbm, gain_ref, wq_hbm, wk_hbm, wv_hbm, out_ref, x_v, wq_v, wk_v, wv_v, st_own, st_in, nrm, pp, dr, own, xs, xr, ld_sem, send_sem, st_sem, d_sem, x_sem):
    mx = lax.axis_index("mx")
    xi, ci = mx // 2, mx % 2
    partner, xpeer = 2 * xi + (1 - ci), 2 * (1 - xi) + ci
    loads = [pltpu.make_async_copy(s, d, ld_sem.at[i]) for i, (s, d) in enumerate([(x_hbm, x_v), (wq_hbm, wq_v), (wk_hbm, wk_v), (wv_hbm, wv_v)])]
    for ld in loads:
        ld.start()
    barrier = pltpu.get_barrier_semaphore()
    for d in range(1, 4):
        pl.semaphore_signal(barrier, inc=1, device_id={"mx": (mx + d) % 4}, device_id_type=MESH)
    pl.semaphore_wait(barrier, 3)

    rows = x_v.shape[0]
    loads[0].wait()
    blocks = []
    for k in range(rows // 8):
        v = x_v[8 * k:8 * k + 8, :].astype(jnp.float32)
        blocks.append(jnp.sum(v * v, axis=1, keepdims=True))
    tile = pack_column(blocks)
    st_own[...] = tile
    st_in[mx] = tile
    for d in range(1, 4):
        rcopy(st_own, st_in.at[mx], send_sem.at[0], st_sem, {"mx": (mx + d) % 4}).start()
    for ld in loads[1:]:
        ld.wait()
    rcopy(st_in.at[pl.ds(0, 3)], st_in.at[pl.ds(0, 3)], send_sem.at[0], st_sem, {"mx": partner}).wait()
    total = st_in[0] + st_in[1] + st_in[2] + st_in[3]
    scale = lax.rsqrt(total / hidden + NORM_EPS)
    gain = gain_ref[...].astype(jnp.float32)
    for k in range(0, rows // 8, 2):
        col = jnp.concatenate([unpack_column(scale, k), unpack_column(scale, k + 1)], axis=0)
        nrm[8 * k:8 * k + 16, :] = (x_v[8 * k:8 * k + 16, :].astype(jnp.float32) * col * gain).astype(jnp.bfloat16)

    lhs = nrm[...]
    part = rows // 4
    off = 0
    for w in (wq_v, wk_v, wv_v):
        width = w.shape[1]
        for c0 in range(0, width, 256):
            cw = min(256, width - c0)
            r = jnp.dot(lhs, w[:, c0:c0 + cw], preferred_element_type=jnp.float32).astype(jnp.bfloat16)
            for m in range(4):
                pp[m % 2, m // 2, :, off + c0:off + c0 + cw] = r[m * part:(m + 1) * part]
        off += width
    rcopy(pp.at[1 - ci], dr, send_sem.at[1], d_sem, {"mx": partner}).start()
    rcopy(pp.at[1 - ci], dr, send_sem.at[1], d_sem, {"mx": partner}).wait_recv()
    xs[...] = (pp[ci, 1 - xi].astype(jnp.float32) + dr[1 - xi].astype(jnp.float32)).astype(jnp.bfloat16)
    out = rcopy(xs, xr, send_sem.at[2], x_sem, {"mx": xpeer})
    out.start()
    own[...] = pp[ci, xi].astype(jnp.float32) + dr[xi].astype(jnp.float32)
    out.wait_recv()
    out_ref[...] = own[...] + xr[...].astype(jnp.float32)
    out.wait_send()
    rcopy(pp.at[1 - ci], dr, send_sem.at[1], d_sem, {"mx": partner}).wait_send()


def qkv_call(x_in, gain, w_q, w_k, w_v, hidden):
    rows, cols = x_in.shape
    width = w_q.shape[1] + w_k.shape[1] + w_v.shape[1]
    bf, f32 = jnp.bfloat16, jnp.float32
    any_spec, vmem = pl.BlockSpec(memory_space=pl.ANY), pl.BlockSpec(memory_space=pltpu.VMEM)
    part = rows // 4
    return pl.pallas_call(
        functools.partial(qkv_kernel, hidden),
        name="qkv",
        out_shape=jax.ShapeDtypeStruct((part, width), f32),
        in_specs=[any_spec, vmem, any_spec, any_spec, any_spec],
        out_specs=vmem,
        scratch_shapes=[
            pltpu.VMEM((rows, cols), bf), pltpu.VMEM(w_q.shape, bf), pltpu.VMEM(w_k.shape, bf), pltpu.VMEM(w_v.shape, bf),
            pltpu.VMEM((8, 128), f32), pltpu.VMEM((4, 8, 128), f32), pltpu.VMEM((rows, cols), bf),
            pltpu.VMEM((2, 2, part, width), bf), pltpu.VMEM((2, part, width), bf), pltpu.VMEM((part, width), f32),
            pltpu.VMEM((part, width), bf), pltpu.VMEM((part, width), bf),
            pltpu.SemaphoreType.DMA((4,)), pltpu.SemaphoreType.DMA((3,)), pltpu.SemaphoreType.DMA, pltpu.SemaphoreType.DMA, pltpu.SemaphoreType.DMA,
        ],
        compiler_params=pltpu.CompilerParams(collective_id=0, has_side_effects=True, vmem_limit_bytes=32 * 1024 * 1024),
    )(x_in, gain, w_q, w_k, w_v)


def mlp_kernel(hidden, x_hbm, gain_ref, attn_ref, wo_hbm, wg_hbm, wu_hbm, wd_hbm, out_ref,
               x_v, wo_v, wg_v, wu_v, wd_v, attn_v, p1, rs1, mp, ag1, st_own, st_in, h2,
               pp, dr, own, xs, xr, act, dacc, p2, rs2, mo, ag2,
               ld_sem, send_sem, at_sem, rs1_sem, ag1_sem, st_sem, rs2_sem, ag2_sem, d_sem, x_sem, ax_sem, ad_sem, af_sem):
    my, mx = lax.axis_index("my"), lax.axis_index("mx")
    n_my = 8
    xi, ci = mx // 2, mx % 2
    zi, yi = my // 2, my % 2
    partner, xpeer = 2 * xi + (1 - ci), 2 * (1 - xi) + ci
    core_dev, x_dev = {"mx": partner}, {"mx": xpeer}
    n_h = h2.shape[0]
    ff = wg_v.shape[1]
    n_j = pl.cdiv(ff, CHUNK)
    tail = ff - CHUNK * (n_j - 1)
    steps = n_h * n_j
    half = x_v.shape[1] // 2
    brows = attn_ref.shape[0]
    f32, bf = jnp.float32, jnp.bfloat16

    loads = [pltpu.make_async_copy(s, d, ld_sem.at[i]) for i, (s, d) in enumerate([
        (wo_hbm, wo_v), (x_hbm, x_v), (wg_hbm, wg_v), (wu_hbm, wu_v), (wd_hbm, wd_v.at[pl.ds(0, ff)])])]
    for ld in loads:
        ld.start()
    barrier = pltpu.get_barrier_semaphore()
    for d in range(1, 4):
        pl.semaphore_signal(barrier, inc=1, device_id={"mx": (mx + d) % 4}, device_id_type=MESH)
    for d in range(1, n_my):
        pl.semaphore_signal(barrier, inc=1, device_id={"my": (my + d) % n_my}, device_id_type=MESH)
    pl.semaphore_wait(barrier, 3 + n_my - 1)

    my_rows = pl.ds(pl.multiple_of(mx * brows, 16), brows)
    for d in range(1, 4):
        rcopy(attn_ref, attn_v.at[my_rows], send_sem.at[0], at_sem, {"mx": (mx + d) % 4}).start()
    attn_v[my_rows, :] = attn_ref[...]
    dacc[...] = jnp.zeros_like(dacc)
    wd_v[ff:, :] = jnp.zeros((wd_v.shape[0] - ff, wd_v.shape[1]), bf)
    loads[0].wait()
    gathered = attn_v.at[pl.ds(0, 3 * brows)]
    rcopy(gathered, gathered, send_sem.at[0], at_sem, core_dev).wait()

    for y in range(2):
        r = jnp.dot(attn_v[...], wo_v[:, y * half:(y + 1) * half], preferred_element_type=f32).astype(bf)
        for h in range(n_h):
            for z in range(4):
                r0 = h * ROWS + z * 16
                p1[h, 2 * z + y] = r[r0:r0 + 16]

    def send_rs(p, rs, h, ssem, rsem):
        for d in range(1, n_my):
            peer = (my + d) % n_my
            rcopy(p.at[h, peer], rs.at[h, d - 1], ssem, rsem.at[h], {"my": peer}).start()

    def finish_rs(p, rs, h, ssem, rsem, base):
        rcopy(rs.at[h], rs.at[h], ssem, rsem.at[h], {"my": my}).wait_recv()
        total = p[h, my].astype(f32)
        for i in range(n_my - 1):
            total += rs[h, i].astype(f32)
        return (base + total).astype(bf)

    def send_ag(piece, ag, h, ssem, rsem):
        for d in range(1, n_my):
            rcopy(piece.at[h], ag.at[h, my], ssem, rsem.at[h], {"my": (my + d) % n_my}).start()

    def wait_ag(ag, h, ssem, rsem):
        seven = ag.at[h, pl.ds(0, n_my - 1)]
        rcopy(seven, seven, ssem, rsem.at[h], {"my": my}).wait_recv()

    def rs1_send(h):
        send_rs(p1, rs1, h, send_sem.at[1], rs1_sem)

    def rs1_finish(h):
        r0 = pl.multiple_of(h * ROWS + zi * 16, 16)
        base = x_v[pl.ds(r0, 16), pl.ds(pl.multiple_of(yi * half, 128), half)].astype(f32)
        m = finish_rs(p1, rs1, h, send_sem.at[1], rs1_sem, base)
        mp[h] = m
        ag1[h, my] = m
        send_ag(mp, ag1, h, send_sem.at[2], ag1_sem)

    def stat_send(h):
        wait_ag(ag1, h, send_sem.at[2], ag1_sem)
        blocks = []
        for z in range(4):
            a, b = ag1[h, 2 * z].astype(f32), ag1[h, 2 * z + 1].astype(f32)
            ss = jnp.sum(a * a, axis=1, keepdims=True) + jnp.sum(b * b, axis=1, keepdims=True)
            blocks += [ss[:8], ss[8:]]
        tile = pack_column(blocks)
        st_own[h] = tile
        st_in[h, mx] = tile
        for d in range(1, 4):
            rcopy(st_own.at[h], st_in.at[h, mx], send_sem.at[3], st_sem.at[h], {"mx": (mx + d) % 4}).start()

    def norm(h):
        three = st_in.at[h, pl.ds(0, 3)]
        rcopy(three, three, send_sem.at[3], st_sem.at[h], core_dev).wait_recv()
        total = st_in[h, 0] + st_in[h, 1] + st_in[h, 2] + st_in[h, 3]
        scale = lax.rsqrt(total / hidden + NORM_EPS)
        for z in range(4):
            col = jnp.concatenate([unpack_column(scale, 2 * z), unpack_column(scale, 2 * z + 1)], axis=0)
            for y in range(2):
                gain = gain_ref[:, y * half:(y + 1) * half].astype(f32)
                h2[h, 16 * z:16 * z + 16, y * half:(y + 1) * half] = (ag1[h, 2 * z + y].astype(f32) * col * gain).astype(bf)

    def stage_a(s):
        h, j = s // n_j, s % n_j

        def put(val, lo, width):
            for m in range(4):
                pp[s, m % 2, m // 2, :, lo:lo + width] = val[16 * m:16 * m + 16]

        @pl.when(j < n_j - 1)
        def _():
            cols = pl.ds(pl.multiple_of(j * CHUNK, CHUNK), CHUNK)
            lhs = h2[h]
            put(jnp.dot(lhs, wg_v[:, cols], preferred_element_type=f32).astype(bf), 0, CHUNK)
            put(jnp.dot(lhs, wu_v[:, cols], preferred_element_type=f32).astype(bf), CHUNK, CHUNK)

        @pl.when(j == n_j - 1)
        def _():
            lhs = h2[h]
            fill = (tail // 128) * 128
            for i, w in enumerate((wg_v, wu_v)):
                if fill < CHUNK:
                    put(jnp.zeros((ROWS, CHUNK - fill), bf), i * CHUNK + fill, CHUNK - fill)
                put(jnp.dot(lhs, w[:, CHUNK * (n_j - 1):ff], preferred_element_type=f32).astype(bf), i * CHUNK, tail)

        rcopy(pp.at[s, 1 - ci], dr.at[s], send_sem.at[4], d_sem.at[s], core_dev).start()

    def stage_b(s):
        rcopy(pp.at[s, 1 - ci], dr.at[s], send_sem.at[4], d_sem.at[s], core_dev).wait_recv()
        xs[s] = (pp[s, ci, 1 - xi].astype(f32) + dr[s, 1 - xi].astype(f32)).astype(bf)
        rcopy(xs.at[s], xr.at[s], send_sem.at[5], x_sem.at[s], x_dev).start()
        own[s] = pp[s, ci, xi].astype(f32) + dr[s, xi].astype(f32)

    def stage_c(s):
        rcopy(xs.at[s], xr.at[s], send_sem.at[5], x_sem.at[s], x_dev).wait_recv()
        g = own[s, :, :CHUNK] + xr[s, :, :CHUNK].astype(f32)
        u = own[s, :, CHUNK:] + xr[s, :, CHUNK:].astype(f32)
        act[s, mx] = (jax.nn.silu(g) * u).astype(bf)
        rcopy(act.at[s, mx], act.at[s, mx], send_sem.at[6], ax_sem.at[s], x_dev).start()
        rcopy(act.at[s, mx], act.at[s, mx], send_sem.at[7], ad_sem.at[s], core_dev).start()

    def stage_d(s):
        rcopy(act.at[s, xpeer], act.at[s, xpeer], send_sem.at[6], ax_sem.at[s], x_dev).wait_recv()
        rcopy(act.at[s, xpeer], act.at[s, xpeer], send_sem.at[8], af_sem.at[s], core_dev).start()

    def stage_e(s):
        h, j = s // n_j, s % n_j
        rcopy(act.at[s, 0], act.at[s, 0], send_sem.at[7], ad_sem.at[s], core_dev).wait_recv()
        rcopy(act.at[s, 0], act.at[s, 0], send_sem.at[8], af_sem.at[s], core_dev).wait_recv()
        lhs = act[s].reshape(ROWS, CHUNK)
        dacc[h] += jnp.dot(lhs, wd_v[pl.ds(pl.multiple_of(j * CHUNK, CHUNK), CHUNK), :], preferred_element_type=f32)

    def rs2_send(h):
        for z in range(4):
            for y in range(2):
                p2[h, 2 * z + y] = dacc[h, 16 * z:16 * z + 16, y * half:(y + 1) * half].astype(bf)
        send_rs(p2, rs2, h, send_sem.at[9], rs2_sem)

    def rs2_finish(h):
        o = finish_rs(p2, rs2, h, send_sem.at[9], rs2_sem, mp[h].astype(f32))
        mo[h] = o
        ag2[h, my] = o
        send_ag(mo, ag2, h, send_sem.at[10], ag2_sem)

    rs1_send(0)
    loads[1].wait()
    rs1_finish(0)
    rs1_send(1)
    stat_send(0)
    for ld in loads[2:4]:
        ld.wait()
    norm(0)

    lag2 = 5

    def body(t, carry):
        h_now, j_now = t // n_j, t % n_j

        @pl.when((h_now + 1 < n_h) & (j_now == 1))
        def _():
            rs1_finish(h_now + 1)

        @pl.when((h_now + 2 < n_h) & (j_now == 2))
        def _():
            rs1_send(h_now + 2)

        @pl.when((h_now + 1 < n_h) & (j_now == 4))
        def _():
            stat_send(h_now + 1)

        @pl.when((t < steps) & (j_now == 0) & (t > 0))
        def _():
            norm(h_now)

        @pl.when(t < steps)
        def _():
            stage_a(t)

        @pl.when((t >= LAG_B) & (t < steps + LAG_B))
        def _():
            stage_b(t - LAG_B)

        @pl.when((t >= LAG_C) & (t < steps + LAG_C))
        def _():
            stage_c(t - LAG_C)

        @pl.when((t >= LAG_D) & (t < steps + LAG_D))
        def _():
            stage_d(t - LAG_D)

        @pl.when(t == LAG_E)
        def _():
            loads[4].wait()

        @pl.when(t >= LAG_E)
        def _():
            s = t - LAG_E
            stage_e(s)

            @pl.when(s % n_j == n_j - 1)
            def _():
                rs2_send(s // n_j)

        @pl.when((t >= LAG_E + n_j - 1 + lag2) & ((t - LAG_E - (n_j - 1) - lag2) % n_j == 0))
        def _():
            rs2_finish((t - LAG_E - (n_j - 1) - lag2) // n_j)

        return carry

    total_t = steps + LAG_E
    lax.fori_loop(0, total_t, body, 0)
    done = len([h for h in range(n_h) if LAG_E + n_j - 1 + lag2 + h * n_j < total_t])
    for h in range(done, n_h):
        rs2_finish(h)
    for h in range(n_h):
        wait_ag(ag2, h, send_sem.at[10], ag2_sem)
        for z in range(4):
            for y in range(2):
                r0 = h * ROWS + z * 16
                out_ref[r0:r0 + 16, y * half:(y + 1) * half] = ag2[h, 2 * z + y]
    for k, ref in ((1, rs1), (2, rs1), (3, st_in.at[:, pl.ds(0, 3)]), (4, dr), (5, xs), (6, act.at[:, 0]), (7, act.at[:, 0]), (8, act.at[:, 0]), (9, rs2), (10, rs2)):
        rcopy(ref, ref, send_sem.at[k], at_sem, core_dev).wait_send()


def mlp_call(x_in, gain, attn, w_o, w_gate, w_up, w_down, hidden):
    rows, cols = x_in.shape
    ff = w_gate.shape[1]
    n_j = pl.cdiv(ff, CHUNK)
    n_h = rows // ROWS
    steps = n_h * n_j
    half = cols // 2
    bf, f32 = jnp.bfloat16, jnp.float32
    any_spec, vmem = pl.BlockSpec(memory_space=pl.ANY), pl.BlockSpec(memory_space=pltpu.VMEM)
    dma = pltpu.SemaphoreType.DMA
    return pl.pallas_call(
        functools.partial(mlp_kernel, hidden),
        name="mlp",
        out_shape=jax.ShapeDtypeStruct((rows, cols), bf),
        in_specs=[any_spec, vmem, vmem, any_spec, any_spec, any_spec, any_spec],
        out_specs=vmem,
        scratch_shapes=[
            pltpu.VMEM((rows, cols), bf), pltpu.VMEM(w_o.shape, bf), pltpu.VMEM(w_gate.shape, bf), pltpu.VMEM(w_up.shape, bf),
            pltpu.VMEM((n_j * CHUNK, cols), bf), pltpu.VMEM((rows, attn.shape[1]), bf),
            pltpu.VMEM((n_h, 8, 16, half), bf), pltpu.VMEM((n_h, 7, 16, half), bf), pltpu.VMEM((n_h, 16, half), bf), pltpu.VMEM((n_h, 8, 16, half), bf),
            pltpu.VMEM((n_h, 8, 128), f32), pltpu.VMEM((n_h, 4, 8, 128), f32), pltpu.VMEM((n_h, ROWS, cols), bf),
            pltpu.VMEM((steps, 2, 2, 16, 2 * CHUNK), bf), pltpu.VMEM((steps, 2, 16, 2 * CHUNK), bf), pltpu.VMEM((steps, 16, 2 * CHUNK), f32),
            pltpu.VMEM((steps, 16, 2 * CHUNK), bf), pltpu.VMEM((steps, 16, 2 * CHUNK), bf), pltpu.VMEM((steps, 4, 16, CHUNK), bf),
            pltpu.VMEM((n_h, ROWS, cols), f32),
            pltpu.VMEM((n_h, 8, 16, half), bf), pltpu.VMEM((n_h, 7, 16, half), bf), pltpu.VMEM((n_h, 16, half), bf), pltpu.VMEM((n_h, 8, 16, half), bf),
            dma((5,)), dma((11,)), dma, dma((n_h,)), dma((n_h,)), dma((n_h,)), dma((n_h,)), dma((n_h,)),
            dma((steps,)), dma((steps,)), dma((steps,)), dma((steps,)), dma((steps,)),
        ],
        compiler_params=pltpu.CompilerParams(collective_id=1, has_side_effects=True, vmem_limit_bytes=VMEM_LIMIT),
    )(x_in, gain, attn, w_o, w_gate, w_up, w_down)


def apply_rotary(vectors, positions):
    half_dim = HEAD // 2
    inv_freq = ROPE_THETA ** (-2.0 * jnp.arange(half_dim, dtype=jnp.float32) / HEAD)
    angles = positions.astype(jnp.float32)[:, None, None] * inv_freq
    cos_tab = jnp.cos(angles)
    sin_tab = jnp.sin(angles)
    lower_half = vectors[..., :half_dim]
    upper_half = vectors[..., half_dim:]
    return jnp.concatenate([lower_half * cos_tab - upper_half * sin_tab, upper_half * cos_tab + lower_half * sin_tab], axis=-1)


def attend_local(q_rot, k_cache_out, v_cache_out, seq_lens):
    row_count, seq_len, kv_heads, _ = k_cache_out.shape
    q_heads = q_rot.shape[1]
    q_grouped = q_rot.reshape(row_count, kv_heads, q_heads // kv_heads, HEAD)
    scores = jnp.einsum("bkgd,bskd->bkgs", q_grouped, k_cache_out, preferred_element_type=jnp.float32) * HEAD ** -0.5
    visible = (jnp.arange(seq_len)[None, :] <= seq_lens[:, None])[:, None, None, :]
    scores = jnp.where(visible, scores, -jnp.inf)
    weights = jnp.exp(scores - jnp.max(scores, axis=-1, keepdims=True))
    weight_sum = jnp.sum(weights, axis=-1, keepdims=True)
    weighted = jnp.einsum("bkgs,bskd->bkgd", weights.astype(jnp.bfloat16), v_cache_out, preferred_element_type=jnp.float32)
    return (weighted / weight_sum).astype(jnp.bfloat16).reshape(row_count, q_heads * HEAD)


def solution(mesh):
    mx_size = mesh.shape["mx"]
    act_spec = P(None, "mx")
    cache_spec = P("mx", None, "my", None)
    in_specs = (act_spec, P("mx"), P("mx"), P("mx"), P("mx", "my"), P("my"), P("mx", "my"), P("my"), P("mx", "my"), P("my"), P("my", "mx"), P("mx", "my"), P("mx", "my"), P("my", "mx"), cache_spec, cache_spec)
    out_specs = (act_spec, cache_spec, cache_spec)

    def local_layer(x_in, seq_lens, gain_attn, gain_mlp, w_q, b_q, w_k, b_k, w_v, b_v, w_o, w_gate, w_up, w_down, k_cache, v_cache):
        hidden = x_in.shape[1] * mx_size
        projected = qkv_call(x_in, gain_attn[None], w_q, w_k, w_v, hidden)
        q_cols = w_q.shape[1]
        kv_cols = w_k.shape[1]
        row_count = projected.shape[0]
        kv_heads = kv_cols // HEAD
        q_vals = projected[:, :q_cols] + b_q.astype(jnp.float32)
        k_vals = projected[:, q_cols:q_cols + kv_cols] + b_k.astype(jnp.float32)
        v_vals = projected[:, q_cols + kv_cols:] + b_v.astype(jnp.float32)
        q_rot = apply_rotary(q_vals.reshape(row_count, q_cols // HEAD, HEAD), seq_lens).astype(jnp.bfloat16)
        k_rot = apply_rotary(k_vals.reshape(row_count, kv_heads, HEAD), seq_lens).astype(jnp.bfloat16)
        v_new = v_vals.reshape(row_count, kv_heads, HEAD).astype(jnp.bfloat16)
        at_slot = (jnp.arange(k_cache.shape[1])[None, :] == seq_lens[:, None])[:, :, None, None]
        k_cache_out = jnp.where(at_slot, k_rot[:, None], k_cache)
        v_cache_out = jnp.where(at_slot, v_new[:, None], v_cache)
        attn_rows = attend_local(q_rot, k_cache_out, v_cache_out, seq_lens)
        x_out = mlp_call(x_in, gain_mlp[None], attn_rows, w_o, w_gate, w_up, w_down, hidden)
        return x_out, k_cache_out, v_cache_out

    return jax.shard_map(local_layer, mesh=mesh, in_specs=in_specs, out_specs=out_specs, check_vma=False)
```

time: 306 us -> 143 us (0.47)
  waiting for transfers between devices: 225 us -> 0 us
  Pallas kernels: 0 us -> 90.9 us
  local copies, waits for them, and re-layouts: 0.71 us -> 33.7 us
  matrix products: 29.1 us -> 5.3 us
  blocking collectives: 19.8 us -> 0 us
  between operations: 14 us -> 0.75 us
  other arithmetic: 16.9 us -> 11.2 us
    psum x3 -> x0, waiting for transfers between devices: 204 us -> none  [the longest x1 72.4 us: local_layer(): lax.psum(jnp.dot(hidden_act, w_down, preferred_element_type=jnp.float32)....]
    pallas_call x0 -> x2, Pallas kernels: none -> 90.9 us  [the longest x1 78.2 us: mlp_call(): pl.pallas_call(functools.partial(mlp_kernel, hidden), name='mlp', out_sha...]
    unnamed x21 -> x18, local copies, waits for them, and re-layouts: 0.69 us -> 32.3 us
    dot_general x7 -> x0, matrix products: 26.3 us -> none  [the longest x1 6.78 us: local_layer(): jnp.dot(hidden_act, w_down, preferred_element_type=jnp.float32)]
    reduce_scatter x1 -> x0, waiting for transfers between devices: 20.5 us -> none  [local_layer(): lax.psum_scatter(partials, 'mx', scatter_dimension=0, tiled=True)]
    psum x2 -> x0, blocking collectives: 14.1 us -> none  [the longest x1 8.4 us: local_layer(): attn_sq = lax.psum(jnp.sum(x_f32 * x_f32, axis=1, keepdims=True), 'mx')]
    all_gather x1 -> x0, blocking collectives: 5.74 us -> none  [local_layer(): attn_all = lax.all_gather(attn_rows, 'mx', axis=0, tiled=True)]
    convert_element_type x5 -> x0, other arithmetic: 5.61 us -> none  [the longest x1 2.09 us: local_layer(): gate_up = lax.psum(jnp.concatenate([jnp.dot(normed_mlp, w_gate, preferred...]
  transfers between devices with their start and end apart: 4 -> 0, of which waited for: 4 -> 0; matrix products, arithmetic and copies ran while one was open for 0% -> 0% of each run, Pallas kernels for 0% -> 0%
where the time goes in v1:
time: 143 us; the launch traced here: 142 us
  Pallas kernels  90.9 us (64%)
  local copies, waits for them, and re-layouts  33.7 us (24%)
  other arithmetic  11.2 us (8%)
  matrix products  5.3 us (4%)
    pallas_call x1, Pallas kernels, mlp_call(): pl.pallas_call(functools.partial(mlp_kernel, hidden), name='mlp', out_sha...  78.2 us
    unnamed x18, local copies, waits for them, and re-layouts  32.3 us
    pallas_call x1, Pallas kernels, qkv_call(): pl.pallas_call(functools.partial(qkv_kernel, hidden), name='qkv', out_sha...  12.7 us
    select_n x1, other arithmetic, local_layer(): k_cache_out = jnp.where(at_slot, k_rot[:, None], k_cache)  7.68 us
    dot_general x1, matrix products, attend_local(): jnp.einsum('bkgd,bskd->bkgs', q_grouped, k_cache_out, preferred_element_t...  4.34 us

profile of v1, /device:TPU:0, one launch (start us, length us, event | category | flops | bytes accessed | tf_op | source)
XLA Modules:
  0.0 141.9 jit_solution(12185075617627071373)
XLA Ops:
  0.6 0.7 broadcast_in_dim.61.gain_ref
  1.3 1.0 copy-done
  2.4 0.0 copy-start.1
  2.4 1.4 %copy-done.1 = bf16[1280,640]{1,0:T(8,128)(2,1)S(1)} copy-done((bf16[1280,640]{1,0:T(8,128)(2,1)S(1)}, bf16[1280,640]{1,0:T(8,128)(2,1)}, u32[]{:S(2)}) %copy-start.1) | copy-done | bytes 1638424
  3.8 0.0 copy-start.2
  3.8 1.0 copy-done.2
  4.8 0.0 copy-start.3
  4.8 1.0 copy-done.3
  5.7 12.7 %qkv.1 = f32[48,896]{1,0:T(8,128)S(1)} custom-call(bf16[192,1280]{1,0:T(8,128)(2,1)S(1)} %copy-done, bf16[1,1280]{1,0:T(2,128)(2,1)S(1)} %broadcast_in_dim.61.gain_ref, bf16[1280,640]{1,0:T(8,128)(2,1)S(1)} %copy-done.1, bf16[1280,128]{1,0:T(8,128)(2,1)S(1)} %copy-done.2, bf16[1280,128]{1,0:T(8,128)(2,1)S(1)} %copy-done.3), custom_call_target="tpu_custom_call" | custom-call | tf_op jit(solution)/shard_map/qkv/pallas_call | solution.py:102
  18.5 0.7 convert_element_type.37
  19.1 0.7 convert_element_type.39
  19.8 0.7 convert_element_type.36
  20.5 0.2 fusion.32
  20.7 0.1 pad_maximum_fusion
  20.7 0.7 iota_compare_fusion.1
  21.5 0.0 copy-start.6
  21.5 7.7 %broadcast_select_fusion.1 = (bf16[48,384,1,128]{3,1,2,0:T(8,128)(2,1)}, bf16[48,384,1,128]{3,1,2,0:T(8,128)(2,1)}) fusion(bf16[48,384,1,128]{3,1,2,0:T(8,128)(2,1)} %param.30, pred[48,384]{1,0:T(8,128)(4,1)S(1)} %get-tuple-element.14, bf16[48,128]{1,0:T(8,128)(2,1)S(1)} %pad_maximum_fusion, bf16[48,384,1,128]{3,1,2,0:T(8,128)(2,1)} %param.31, ...), kind=kLoop, calls=%fused_computation.5 | loop fusion | flops 4718592 | bytes 18917376 | tf_op jit(solution)/shard_map/jit(_where)/select_n | solution.py:440
  29.2 0.2 multiply_cosine_fusion.1
  29.3 0.0 copy-done.6
  29.4 0.0 copy-start.4
  29.4 0.1 subtract_convert_fusion
  29.6 4.3 %fusion.34 = (f32[48,5]{1,0:T(8,128)S(1)}, f32[48,5,384]{2,1,0:T(8,128)S(1)}) fusion(bf16[48,384,1,128]{3,1,2,0:T(8,128)(2,1)} %get-tuple-element.21, bf16[48,5,64]{2,1,0:T(8,128)(2,1)S(1)} %get-tuple-element.4, bf16[48,5,64]{2,1,0:T(8,128)(2,1)S(1)} %get-tuple-element.3, pred[48,384]{1,0:T(8,128)(4,1)S(1)} %get-tuple-element.13), kind=kOutput, calls=%fused_computation.42 | convolution fusion | flops 23992080 | bytes 5168064 | tf_op jit(solution)/shard_map/bkgd,bskd->bkgs/dot_general | solution.py:410
  33.9 0.2 fusion.16
  34.2 0.0 copy-done.4
  34.2 1.0 fusion.13
  35.1 0.7 copy.25
  35.8 12.7 %copy.21.wg_hbm = bf16[1280,3424]{1,0:T(8,128)(2,1)} copy(bf16[1280,3424]{0,1:T(8,128)(2,1)} %param.27) | data formatting | bytes 17530880 | tf_op args[11]
  48.5 12.7 %copy.22.wu_hbm = bf16[1280,3424]{1,0:T(8,128)(2,1)} copy(bf16[1280,3424]{0,1:T(8,128)(2,1)} %param.28) | data formatting | bytes 17530880 | tf_op args[12]
  61.2 0.0 copy-done.5
  61.2 0.6 broadcast_in_dim.59.gain_ref
  61.8 78.2 %mlp.1 = bf16[192,1280]{1,0:T(8,128)(2,1)} custom-call(bf16[192,1280]{1,0:T(8,128)(2,1)} %x_hbm.3, bf16[1,1280]{1,0:T(2,128)(2,1)} %broadcast_in_dim.59.gain_ref, bf16[48,640]{1,0:T(8,128)(2,1)} %bitcast.27, bf16[640,1280]{1,0:T(8,128)(2,1)} %wo_hbm.1, bf16[1280,3424]{1,0:T(8,128)(2,1)} %copy.21.wg_hbm, bf16[1280,3424]{1,0:T(8,128)(2,1)} %copy.22.wu_hbm, ...), custom_call_target="tpu_custom_call" | custom-call | tf_op jit(solution)/shard_map/mlp/pallas_call | solution.py:373
  140.0 1.8 %copy.27 = bf16[192,1280]{1,0:T(8,128)(2,1)} copy(bf16[192,1280]{1,0:T(8,128)(2,1)} %mlp.1) | data formatting | bytes 983040
  (7 shorter events, 0.1 us)
Async XLA Ops:
  1.3 1.0 copy-start
  2.4 1.4 %copy-start.1 = (bf16[1280,640]{1,0:T(8,128)(2,1)S(1)}, bf16[1280,640]{1,0:T(8,128)(2,1)}, u32[]{:S(2)}) copy-start(bf16[1280,640]{1,0:T(8,128)(2,1)} %wq_hbm.1) | copy-start | bytes 4915204
  3.8 1.0 copy-start.2
  4.8 1.0 copy-start.3
  21.5 7.9 %copy-start.6 = (bf16[640]{0:T(1024)(128)(2,1)S(1)}, bf16[640]{0:T(1024)(128)(2,1)}, u32[]{:S(2)}) copy-start(bf16[640]{0:T(1024)(128)(2,1)} %param.21) | copy-start | bytes 3844
  29.4 4.7 %copy-start.4 = (bf16[48,384,1,128]{3,1,2,0:T(8,128)(2,1)S(1)}, bf16[48,384,1,128]{3,1,2,0:T(8,128)(2,1)}, u32[]{:S(2)}) copy-start(bf16[48,384,1,128]{3,1,2,0:T(8,128)(2,1)} %get-tuple-element.22) | copy-start | bytes 14155780
  48.5 12.7 %copy-start.5 = (bf16[1280]{0:T(1024)(128)(2,1)S(1)}, bf16[1280]{0:T(1024)(128)(2,1)}, u32[]{:S(2)}) copy-start(bf16[1280]{0:T(1024)(128)(2,1)} %param.19) | copy-start | bytes 7684

commit v2 on v1

--- a/solution.py
+++ b/solution.py
@@ -2,6 +2,7 @@
 
 import jax
 import jax.numpy as jnp
+import numpy as np
 from jax import lax
 from jax.experimental import pallas as pl
 from jax.experimental.pallas import tpu as pltpu
@@ -65,7 +66,7 @@
     rcopy(st_in.at[pl.ds(0, 3)], st_in.at[pl.ds(0, 3)], send_sem.at[0], st_sem, {"mx": partner}).wait()
     total = st_in[0] + st_in[1] + st_in[2] + st_in[3]
     scale = lax.rsqrt(total / hidden + NORM_EPS)
-    gain = gain_ref[...].astype(jnp.float32)
+    gain = gain_ref[...].astype(jnp.float32).reshape(1, x_v.shape[1])
     for k in range(0, rows // 8, 2):
         col = jnp.concatenate([unpack_column(scale, k), unpack_column(scale, k + 1)], axis=0)
         nrm[8 * k:8 * k + 16, :] = (x_v[8 * k:8 * k + 16, :].astype(jnp.float32) * col * gain).astype(jnp.bfloat16)
@@ -112,7 +113,7 @@
             pltpu.VMEM((part, width), bf), pltpu.VMEM((part, width), bf),
             pltpu.SemaphoreType.DMA((4,)), pltpu.SemaphoreType.DMA((3,)), pltpu.SemaphoreType.DMA, pltpu.SemaphoreType.DMA, pltpu.SemaphoreType.DMA,
         ],
-        compiler_params=pltpu.CompilerParams(collective_id=0, has_side_effects=True, vmem_limit_bytes=32 * 1024 * 1024),
+        compiler_params=pltpu.CompilerParams(collective_id=0, has_side_effects=True, vmem_limit_bytes=VMEM_LIMIT),
     )(x_in, gain, w_q, w_k, w_v)
 
 
@@ -127,16 +128,15 @@
     partner, xpeer = 2 * xi + (1 - ci), 2 * (1 - xi) + ci
     core_dev, x_dev = {"mx": partner}, {"mx": xpeer}
     n_h = h2.shape[0]
-    ff = wg_v.shape[1]
+    ff = wg_hbm.shape[0]
     n_j = pl.cdiv(ff, CHUNK)
-    tail = ff - CHUNK * (n_j - 1)
     steps = n_h * n_j
     half = x_v.shape[1] // 2
     brows = attn_ref.shape[0]
     f32, bf = jnp.float32, jnp.bfloat16
 
     loads = [pltpu.make_async_copy(s, d, ld_sem.at[i]) for i, (s, d) in enumerate([
-        (wo_hbm, wo_v), (x_hbm, x_v), (wg_hbm, wg_v), (wu_hbm, wu_v), (wd_hbm, wd_v.at[pl.ds(0, ff)])])]
+        (wo_hbm, wo_v), (x_hbm, x_v), (wg_hbm, wg_v.at[pl.ds(0, ff)]), (wu_hbm, wu_v.at[pl.ds(0, ff)]), (wd_hbm, wd_v.at[pl.ds(0, ff)])])]
     for ld in loads:
         ld.start()
     barrier = pltpu.get_barrier_semaphore()
@@ -151,7 +151,8 @@
         rcopy(attn_ref, attn_v.at[my_rows], send_sem.at[0], at_sem, {"mx": (mx + d) % 4}).start()
     attn_v[my_rows, :] = attn_ref[...]
     dacc[...] = jnp.zeros_like(dacc)
-    wd_v[ff:, :] = jnp.zeros((wd_v.shape[0] - ff, wd_v.shape[1]), bf)
+    for w in (wg_v, wu_v, wd_v):
+        w[ff:, :] = jnp.zeros((w.shape[0] - ff, w.shape[1]), bf)
     loads[0].wait()
     gathered = attn_v.at[pl.ds(0, 3 * brows)]
     rcopy(gathered, gathered, send_sem.at[0], at_sem, core_dev).wait()
@@ -215,32 +216,17 @@
         for z in range(4):
             col = jnp.concatenate([unpack_column(scale, 2 * z), unpack_column(scale, 2 * z + 1)], axis=0)
             for y in range(2):
-                gain = gain_ref[:, y * half:(y + 1) * half].astype(f32)
+                gain = gain_ref[pl.ds(y * half, half)].astype(f32).reshape(1, half)
                 h2[h, 16 * z:16 * z + 16, y * half:(y + 1) * half] = (ag1[h, 2 * z + y].astype(f32) * col * gain).astype(bf)
 
     def stage_a(s):
         h, j = s // n_j, s % n_j
-
-        def put(val, lo, width):
+        lhs = h2[h]
+        part_rows = pl.ds(pl.multiple_of(j * CHUNK, CHUNK), CHUNK)
+        for i, w in enumerate((wg_v, wu_v)):
+            val = lax.dot_general(lhs, w[part_rows, :], (((1,), (1,)), ((), ())), preferred_element_type=f32).astype(bf)
             for m in range(4):
-                pp[s, m % 2, m // 2, :, lo:lo + width] = val[16 * m:16 * m + 16]
-
-        @pl.when(j < n_j - 1)
-        def _():
-            cols = pl.ds(pl.multiple_of(j * CHUNK, CHUNK), CHUNK)
-            lhs = h2[h]
-            put(jnp.dot(lhs, wg_v[:, cols], preferred_element_type=f32).astype(bf), 0, CHUNK)
-            put(jnp.dot(lhs, wu_v[:, cols], preferred_element_type=f32).astype(bf), CHUNK, CHUNK)
-
-        @pl.when(j == n_j - 1)
-        def _():
-            lhs = h2[h]
-            fill = (tail // 128) * 128
-            for i, w in enumerate((wg_v, wu_v)):
-                if fill < CHUNK:
-                    put(jnp.zeros((ROWS, CHUNK - fill), bf), i * CHUNK + fill, CHUNK - fill)
-                put(jnp.dot(lhs, w[:, CHUNK * (n_j - 1):ff], preferred_element_type=f32).astype(bf), i * CHUNK, tail)
-
+                pp[s, m % 2, m // 2, :, i * CHUNK:(i + 1) * CHUNK] = val[16 * m:16 * m + 16]
         rcopy(pp.at[s, 1 - ci], dr.at[s], send_sem.at[4], d_sem.at[s], core_dev).start()
 
     def stage_b(s):
@@ -362,7 +348,7 @@
 
 def mlp_call(x_in, gain, attn, w_o, w_gate, w_up, w_down, hidden):
     rows, cols = x_in.shape
-    ff = w_gate.shape[1]
+    ff = w_gate.shape[0]
     n_j = pl.cdiv(ff, CHUNK)
     n_h = rows // ROWS
     steps = n_h * n_j
@@ -377,7 +363,7 @@
         in_specs=[any_spec, vmem, vmem, any_spec, any_spec, any_spec, any_spec],
         out_specs=vmem,
         scratch_shapes=[
-            pltpu.VMEM((rows, cols), bf), pltpu.VMEM(w_o.shape, bf), pltpu.VMEM(w_gate.shape, bf), pltpu.VMEM(w_up.shape, bf),
+            pltpu.VMEM((rows, cols), bf), pltpu.VMEM(w_o.shape, bf), pltpu.VMEM((n_j * CHUNK, cols), bf), pltpu.VMEM((n_j * CHUNK, cols), bf),
             pltpu.VMEM((n_j * CHUNK, cols), bf), pltpu.VMEM((rows, attn.shape[1]), bf),
             pltpu.VMEM((n_h, 8, 16, half), bf), pltpu.VMEM((n_h, 7, 16, half), bf), pltpu.VMEM((n_h, 16, half), bf), pltpu.VMEM((n_h, 8, 16, half), bf),
             pltpu.VMEM((n_h, 8, 128), f32), pltpu.VMEM((n_h, 4, 8, 128), f32), pltpu.VMEM((n_h, ROWS, cols), bf),
@@ -392,28 +378,101 @@
     )(x_in, gain, attn, w_o, w_gate, w_up, w_down)
 
 
-def apply_rotary(vectors, positions):
-    half_dim = HEAD // 2
-    inv_freq = ROPE_THETA ** (-2.0 * jnp.arange(half_dim, dtype=jnp.float32) / HEAD)
-    angles = positions.astype(jnp.float32)[:, None, None] * inv_freq
+GROUP_ROWS = 8
+
+
+def attn_kernel(seq_ref, proj_ref, bq_ref, bk_ref, bv_ref, freq_ref, k_hbm, v_hbm, attn_ref, ko_hbm, vo_hbm, kc, vc, qs, kn, vn, os, pos, in_sem, out_sem):
+    f32, bf = jnp.float32, jnp.bfloat16
+    rows, seq = kc.shape[0], kc.shape[1]
+    heads = attn_ref.shape[1] // HEAD
+    groups = rows // GROUP_ROWS
+
+    def moves(g, out):
+        part = pl.ds(g * GROUP_ROWS, GROUP_ROWS)
+        pairs, sem = (((kc, ko_hbm), (vc, vo_hbm)), out_sem) if out else (((k_hbm, kc), (v_hbm, vc)), in_sem)
+        return [pltpu.make_async_copy(src.at[part], dst.at[part], sem.at[i, g]) for i, (src, dst) in enumerate(pairs)]
+
+    for g in range(groups):
+        for cp in moves(g, False):
+            cp.start()
+    for b in range(rows):
+        pos[b:b + 1, :] = jnp.full((1, HEAD), seq_ref[b], jnp.int32).astype(f32)
+    angles = pos[...] * freq_ref[...]
+    lower = lax.broadcasted_iota(jnp.int32, (rows, HEAD), 1) < HEAD // 2
     cos_tab = jnp.cos(angles)
     sin_tab = jnp.sin(angles)
-    lower_half = vectors[..., :half_dim]
-    upper_half = vectors[..., half_dim:]
-    return jnp.concatenate([lower_half * cos_tab - upper_half * sin_tab, upper_half * cos_tab + lower_half * sin_tab], axis=-1)
-
-
-def attend_local(q_rot, k_cache_out, v_cache_out, seq_lens):
-    row_count, seq_len, kv_heads, _ = k_cache_out.shape
-    q_heads = q_rot.shape[1]
-    q_grouped = q_rot.reshape(row_count, kv_heads, q_heads // kv_heads, HEAD)
-    scores = jnp.einsum("bkgd,bskd->bkgs", q_grouped, k_cache_out, preferred_element_type=jnp.float32) * HEAD ** -0.5
-    visible = (jnp.arange(seq_len)[None, :] <= seq_lens[:, None])[:, None, None, :]
-    scores = jnp.where(visible, scores, -jnp.inf)
-    weights = jnp.exp(scores - jnp.max(scores, axis=-1, keepdims=True))
-    weight_sum = jnp.sum(weights, axis=-1, keepdims=True)
-    weighted = jnp.einsum("bkgs,bskd->bkgd", weights.astype(jnp.bfloat16), v_cache_out, preferred_element_type=jnp.float32)
-    return (weighted / weight_sum).astype(jnp.bfloat16).reshape(row_count, q_heads * HEAD)
+    sin_tab = jnp.where(lower, -sin_tab, sin_tab)
+
+    def column(c, bias_ref, k):
+        bias = bias_ref[pl.ds(k * HEAD, HEAD)].astype(f32).reshape(1, HEAD)
+        return proj_ref[:, c * HEAD:(c + 1) * HEAD] + bias
+
+    def rotate(v):
+        return (v * cos_tab + pltpu.roll(v, HEAD // 2, 1) * sin_tab).astype(bf).astype(f32)
+
+    qs[...] = jnp.zeros_like(qs)
+    for h in range(heads):
+        qs[:, h, :] = rotate(column(h, bq_ref, h))
+    kn[...] = rotate(column(heads, bk_ref, 0))
+    vn[...] = column(heads + 1, bv_ref, 0)
+
+    def body(g, carry):
+        for cp in moves(g, False):
+            cp.wait()
+        lens, scores = [], []
+        times = lax.broadcasted_iota(jnp.int32, (8, seq), 1)
+        slots = lax.broadcasted_iota(jnp.int32, (16, HEAD), 0)
+        for r in range(GROUP_ROWS):
+            b = g * GROUP_ROWS + r
+            p = seq_ref[b]
+            slab = pl.multiple_of((p // 16) * 16, 16)
+            hit = slots == p - slab
+            for cache, new in ((kc, kn), (vc, vn)):
+                old = cache[b, pl.ds(slab, 16), :].astype(f32)
+                cache[b, pl.ds(slab, 16), :] = jnp.where(hit, new[pl.ds(b, 1), :], old).astype(bf)
+            s = lax.dot_general(qs[b].astype(bf), kc[b], (((1,), (1,)), ((), ())), preferred_element_type=f32) * HEAD ** -0.5
+            scores.append(jnp.where(times <= p, s, -jnp.inf))
+        s = jnp.concatenate(scores, axis=0)
+        w = jnp.exp(s - jnp.max(s, axis=1, keepdims=True))
+        total = jnp.sum(w, axis=1, keepdims=True)
+        w = w.astype(bf)
+        for r in range(GROUP_ROWS):
+            b = g * GROUP_ROWS + r
+            o = jnp.dot(w[8 * r:8 * r + 8], vc[b], preferred_element_type=f32)
+            os[b] = o / total[8 * r:8 * r + 8]
+        for cp in moves(g, True):
+            cp.start()
+        return carry
+
+    lax.fori_loop(0, groups, body, 0)
+    for h in range(heads):
+        attn_ref[:, h * HEAD:(h + 1) * HEAD] = os[:, h, :].astype(bf)
+    for g in range(groups):
+        for cp in moves(g, True):
+            cp.wait()
+
+
+def attn_call(seq_lens, projected, b_q, b_k, b_v, k_cache, v_cache):
+    rows, seq = k_cache.shape[0], k_cache.shape[1]
+    f32, bf = jnp.float32, jnp.bfloat16
+    freq = (ROPE_THETA ** (-2.0 * np.arange(HEAD // 2) / HEAD)).astype(np.float32)
+    freq = jnp.asarray(np.concatenate([freq, freq])[None])
+    any_spec, vmem, smem = pl.BlockSpec(memory_space=pl.ANY), pl.BlockSpec(memory_space=pltpu.VMEM), pl.BlockSpec(memory_space=pltpu.SMEM)
+    dma = pltpu.SemaphoreType.DMA
+    cache = jax.ShapeDtypeStruct((rows, seq, HEAD), bf)
+    return pl.pallas_call(
+        attn_kernel,
+        name="attn",
+        out_shape=(jax.ShapeDtypeStruct((rows, b_q.shape[0]), bf), cache, cache),
+        in_specs=[smem, vmem, vmem, vmem, vmem, vmem, any_spec, any_spec],
+        out_specs=(vmem, any_spec, any_spec),
+        scratch_shapes=[
+            pltpu.VMEM((rows, seq, HEAD), bf), pltpu.VMEM((rows, seq, HEAD), bf), pltpu.VMEM((rows, 8, HEAD), f32), pltpu.VMEM((rows, HEAD), f32),
+            pltpu.VMEM((rows, HEAD), f32), pltpu.VMEM((rows, 8, HEAD), f32), pltpu.VMEM((rows, HEAD), f32),
+            dma((2, rows // GROUP_ROWS)), dma((2, rows // GROUP_ROWS)),
+        ],
+        compiler_params=pltpu.CompilerParams(vmem_limit_bytes=VMEM_LIMIT),
+    )(seq_lens, projected, b_q, b_k, b_v, freq, k_cache.reshape(rows, seq, HEAD), v_cache.reshape(rows, seq, HEAD))
 
 
 def solution(mesh):
@@ -425,22 +484,10 @@
 
     def local_layer(x_in, seq_lens, gain_attn, gain_mlp, w_q, b_q, w_k, b_k, w_v, b_v, w_o, w_gate, w_up, w_down, k_cache, v_cache):
         hidden = x_in.shape[1] * mx_size
-        projected = qkv_call(x_in, gain_attn[None], w_q, w_k, w_v, hidden)
-        q_cols = w_q.shape[1]
-        kv_cols = w_k.shape[1]
-        row_count = projected.shape[0]
-        kv_heads = kv_cols // HEAD
-        q_vals = projected[:, :q_cols] + b_q.astype(jnp.float32)
-        k_vals = projected[:, q_cols:q_cols + kv_cols] + b_k.astype(jnp.float32)
-        v_vals = projected[:, q_cols + kv_cols:] + b_v.astype(jnp.float32)
-        q_rot = apply_rotary(q_vals.reshape(row_count, q_cols // HEAD, HEAD), seq_lens).astype(jnp.bfloat16)
-        k_rot = apply_rotary(k_vals.reshape(row_count, kv_heads, HEAD), seq_lens).astype(jnp.bfloat16)
-        v_new = v_vals.reshape(row_count, kv_heads, HEAD).astype(jnp.bfloat16)
-        at_slot = (jnp.arange(k_cache.shape[1])[None, :] == seq_lens[:, None])[:, :, None, None]
-        k_cache_out = jnp.where(at_slot, k_rot[:, None], k_cache)
-        v_cache_out = jnp.where(at_slot, v_new[:, None], v_cache)
-        attn_rows = attend_local(q_rot, k_cache_out, v_cache_out, seq_lens)
-        x_out = mlp_call(x_in, gain_mlp[None], attn_rows, w_o, w_gate, w_up, w_down, hidden)
+        projected = qkv_call(x_in, gain_attn, w_q, w_k, w_v, hidden)
+        attn_rows, k_out, v_out = attn_call(seq_lens, projected, b_q, b_k, b_v, k_cache, v_cache)
+        x_out = mlp_call(x_in, gain_mlp, attn_rows, w_o, w_gate.T, w_up.T, w_down, hidden)
+        k_cache_out, v_cache_out = k_out.reshape(k_cache.shape), v_out.reshape(v_cache.shape)
         return x_out, k_cache_out, v_cache_out
 
     return jax.shard_map(local_layer, mesh=mesh, in_specs=in_specs, out_specs=out_specs, check_vma=False)

time: 143 us -> 106 us (0.74); the launches traced: 142 us -> 106 us
  local copies, waits for them, and re-layouts: 33.7 us -> 1.84 us
  Pallas kernels: 90.9 us -> 104 us
  other arithmetic: 11.2 us -> 0 us
  matrix products: 5.3 us -> 0 us
    unnamed x18 -> x1, local copies, waits for them, and re-layouts: 32.3 us -> 1.84 us
    pallas_call x0 -> x1, Pallas kernels: none -> 9.17 us  [attn_call(): pl.pallas_call(attn_kernel, name='attn', out_shape=(jax.ShapeDtypeStruct(...]
    select_n x1 -> x0, other arithmetic: 7.68 us -> none  [local_layer(): k_cache_out = jnp.where(at_slot, k_rot[:, None], k_cache)]
    dot_general x2 -> x0, matrix products: 5.3 us -> none  [the longest x1 4.34 us: attend_local(): jnp.einsum('bkgd,bskd->bkgs', q_grouped, k_cache_out, preferred_element_t...]
    pallas_call x1, Pallas kernels: 78.2 us -> 81.4 us  [mlp_call(): pl.pallas_call(functools.partial(mlp_kernel, hidden), name='mlp', out_sha...]
    convert_element_type x4 -> x0, other arithmetic: 1.98 us -> none  [the longest x1 0.66 us: local_layer(): k_vals = projected[:, q_cols:q_cols + kv_cols] + b_k.astype(jnp.float32)]
where the time goes in v2:
time: 106 us
  Pallas kernels  104 us (98%)
  local copies, waits for them, and re-layouts  1.84 us (2%)
    pallas_call x1, Pallas kernels, mlp_call(): pl.pallas_call(functools.partial(mlp_kernel, hidden), name='mlp', out_sha...  81.4 us
    pallas_call x1, Pallas kernels, qkv_call(): pl.pallas_call(functools.partial(qkv_kernel, hidden), name='qkv', out_sha...  13.4 us
    pallas_call x1, Pallas kernels, attn_call(): pl.pallas_call(attn_kernel, name='attn', out_shape=(jax.ShapeDtypeStruct(...  9.17 us

profile of v2, /device:TPU:0, one launch (start us, length us, event | category | flops | bytes accessed | tf_op | source)
XLA Modules:
  0.0 106.4 jit_solution(10241218822108745826)
XLA Ops:
  0.6 13.4 %qkv.1.proj_ref = f32[48,896]{1,0:T(8,128)} custom-call(bf16[192,1280]{1,0:T(8,128)(2,1)} %x_hbm.3, bf16[1280]{0:T(1024)(128)(2,1)} %gain_ref.2, bf16[1280,640]{1,0:T(8,128)(2,1)} %wq_hbm.1, bf16[1280,128]{1,0:T(8,128)(2,1)} %wk_hbm.1, bf16[1280,128]{1,0:T(8,128)(2,1)} %wv_hbm.1), custom_call_target="tpu_custom_call" | custom-call | tf_op jit(solution)/shard_map/qkv/pallas_call | solution.py:103
  14.0 9.2 %attn.1 = (bf16[48,640]{1,0:T(8,128)(2,1)}, bf16[48,384,128]{2,1,0:T(8,128)(2,1)}, bf16[48,384,128]{2,1,0:T(8,128)(2,1)}) custom-call(s32[48]{0:T(128)} %seq_ref.1, f32[48,896]{1,0:T(8,128)} %qkv.1.proj_ref, bf16[640]{0:T(1024)(128)(2,1)} %bq_ref.1, bf16[128]{0:T(256)(128)(2,1)} %bk_ref.1, bf16[128]{0:T(256)(128)(2,1)} %bv_ref.1, ...), custom_call_target="tpu_custom_call" | custom-call | tf_op jit(solution)/shard_map/attn/pallas_call | solution.py:463
  23.2 81.4 %mlp.1 = bf16[192,1280]{1,0:T(8,128)(2,1)} custom-call(bf16[192,1280]{1,0:T(8,128)(2,1)} %x_hbm.3, bf16[1280]{0:T(1024)(128)(2,1)} %gain_ref.3, bf16[48,640]{1,0:T(8,128)(2,1)} %get-tuple-element.6.attn_ref, bf16[640,1280]{1,0:T(8,128)(2,1)} %wo_hbm.1, bf16[3424,1280]{1,0:T(8,128)(2,1)} %bitcast.10, bf16[3424,1280]{1,0:T(8,128)(2,1)} %bitcast.11, ...), custom_call_target="tpu_custom_call" | custom-call | tf_op jit(solution)/shard_map/mlp/pallas_call | solution.py:359
  104.6 1.8 %copy.23 = bf16[192,1280]{1,0:T(8,128)(2,1)} copy(bf16[192,1280]{1,0:T(8,128)(2,1)} %mlp.1) | data formatting | bytes 983040

commit v3 on v2

--- a/solution.py
+++ b/solution.py
@@ -14,7 +14,7 @@
 MESH = pl.DeviceIdType.MESH
 CHUNK = 512
 ROWS = 64
-LAG_B, LAG_C, LAG_D, LAG_E = 1, 4, 7, 8
+LAG_B, LAG_C, LAG_D, LAG_E, LAG_RS = 1, 4, 7, 8, 8
 VMEM_LIMIT = 66 * 1024 * 1000
 
 
@@ -118,9 +118,9 @@
 
 
 def mlp_kernel(hidden, x_hbm, gain_ref, attn_ref, wo_hbm, wg_hbm, wu_hbm, wd_hbm, out_ref,
-               x_v, wo_v, wg_v, wu_v, wd_v, attn_v, p1, rs1, mp, ag1, st_own, st_in, h2,
+               x_v, wo_v, wg_v, wu_v, wd_v, attn_v, p1, rs1, mp, ag1, st_own, st_in, st_sum, st_all, h2,
                pp, dr, own, xs, xr, act, dacc, p2, rs2, mo, ag2,
-               ld_sem, send_sem, at_sem, rs1_sem, ag1_sem, st_sem, rs2_sem, ag2_sem, d_sem, x_sem, ax_sem, ad_sem, af_sem):
+               ld_sem, send_sem, at_sem, rs1_sem, ag1_sem, st_sem, sg_sem, rs2_sem, ag2_sem, d_sem, x_sem, ax_sem, ad_sem, af_sem):
     my, mx = lax.axis_index("my"), lax.axis_index("mx")
     n_my = 8
     xi, ci = mx // 2, mx % 2
@@ -146,28 +146,31 @@
         pl.semaphore_signal(barrier, inc=1, device_id={"my": (my + d) % n_my}, device_id_type=MESH)
     pl.semaphore_wait(barrier, 3 + n_my - 1)
 
-    my_rows = pl.ds(pl.multiple_of(mx * brows, 16), brows)
-    for d in range(1, 4):
-        rcopy(attn_ref, attn_v.at[my_rows], send_sem.at[0], at_sem, {"mx": (mx + d) % 4}).start()
-    attn_v[my_rows, :] = attn_ref[...]
+    mine = pl.ds(pl.multiple_of(mx * 16, 16), 16)
+    for h in range(n_h):
+        for d in range(1, 4):
+            rcopy(attn_ref.at[pl.ds(16 * h, 16)], attn_v.at[h, mine], send_sem.at[0], at_sem.at[h], {"mx": (mx + d) % 4}).start()
+    for h in range(n_h):
+        attn_v[h, mine, :] = attn_ref[16 * h:16 * h + 16, :]
     dacc[...] = jnp.zeros_like(dacc)
     for w in (wg_v, wu_v, wd_v):
         w[ff:, :] = jnp.zeros((w.shape[0] - ff, w.shape[1]), bf)
     loads[0].wait()
-    gathered = attn_v.at[pl.ds(0, 3 * brows)]
-    rcopy(gathered, gathered, send_sem.at[0], at_sem, core_dev).wait()
-
-    for y in range(2):
-        r = jnp.dot(attn_v[...], wo_v[:, y * half:(y + 1) * half], preferred_element_type=f32).astype(bf)
-        for h in range(n_h):
+
+    zs = (3 - zi, (zi + 2) % 4, zi + 1 - 2 * (zi % 2), zi)
+    peers = [2 * z + y for z in zs for y in (1 - yi, yi)][:-1]
+
+    def project(h):
+        gathered = attn_v.at[h, pl.ds(0, 48)]
+        rcopy(gathered, gathered, send_sem.at[0], at_sem.at[h], core_dev).wait_recv()
+        for y in range(2):
+            r = jnp.dot(attn_v[h], wo_v[:, y * half:(y + 1) * half], preferred_element_type=f32).astype(bf)
             for z in range(4):
-                r0 = h * ROWS + z * 16
-                p1[h, 2 * z + y] = r[r0:r0 + 16]
+                p1[h, 2 * z + y] = r[16 * z:16 * z + 16]
 
     def send_rs(p, rs, h, ssem, rsem):
-        for d in range(1, n_my):
-            peer = (my + d) % n_my
-            rcopy(p.at[h, peer], rs.at[h, d - 1], ssem, rsem.at[h], {"my": peer}).start()
+        for k, peer in enumerate(peers):
+            rcopy(p.at[h, peer], rs.at[h, k], ssem, rsem.at[h], {"my": peer}).start()
 
     def finish_rs(p, rs, h, ssem, rsem, base):
         rcopy(rs.at[h], rs.at[h], ssem, rsem.at[h], {"my": my}).wait_recv()
@@ -177,8 +180,8 @@
         return (base + total).astype(bf)
 
     def send_ag(piece, ag, h, ssem, rsem):
-        for d in range(1, n_my):
-            rcopy(piece.at[h], ag.at[h, my], ssem, rsem.at[h], {"my": (my + d) % n_my}).start()
+        for peer in peers:
+            rcopy(piece.at[h], ag.at[h, my], ssem, rsem.at[h], {"my": peer}).start()
 
     def wait_ag(ag, h, ssem, rsem):
         seven = ag.at[h, pl.ds(0, n_my - 1)]
@@ -188,33 +191,34 @@
         send_rs(p1, rs1, h, send_sem.at[1], rs1_sem)
 
     def rs1_finish(h):
-        r0 = pl.multiple_of(h * ROWS + zi * 16, 16)
+        r0 = pl.multiple_of(zi * brows + h * 16, 16)
         base = x_v[pl.ds(r0, 16), pl.ds(pl.multiple_of(yi * half, 128), half)].astype(f32)
         m = finish_rs(p1, rs1, h, send_sem.at[1], rs1_sem, base)
         mp[h] = m
         ag1[h, my] = m
         send_ag(mp, ag1, h, send_sem.at[2], ag1_sem)
-
-    def stat_send(h):
-        wait_ag(ag1, h, send_sem.at[2], ag1_sem)
-        blocks = []
-        for z in range(4):
-            a, b = ag1[h, 2 * z].astype(f32), ag1[h, 2 * z + 1].astype(f32)
-            ss = jnp.sum(a * a, axis=1, keepdims=True) + jnp.sum(b * b, axis=1, keepdims=True)
-            blocks += [ss[:8], ss[8:]]
-        tile = pack_column(blocks)
+        m = m.astype(f32)
+        ss = jnp.sum(m * m, axis=1, keepdims=True)
+        tile = pack_column([ss[:8], ss[8:]])
         st_own[h] = tile
         st_in[h, mx] = tile
         for d in range(1, 4):
             rcopy(st_own.at[h], st_in.at[h, mx], send_sem.at[3], st_sem.at[h], {"mx": (mx + d) % 4}).start()
 
-    def norm(h):
+    def stat_gather(h):
         three = st_in.at[h, pl.ds(0, 3)]
         rcopy(three, three, send_sem.at[3], st_sem.at[h], core_dev).wait_recv()
         total = st_in[h, 0] + st_in[h, 1] + st_in[h, 2] + st_in[h, 3]
-        scale = lax.rsqrt(total / hidden + NORM_EPS)
+        st_sum[h] = total
+        st_all[h, my] = total
+        send_ag(st_sum, st_all, h, send_sem.at[11], sg_sem)
+
+    def norm(h):
+        wait_ag(st_all, h, send_sem.at[11], sg_sem)
+        wait_ag(ag1, h, send_sem.at[2], ag1_sem)
         for z in range(4):
-            col = jnp.concatenate([unpack_column(scale, 2 * z), unpack_column(scale, 2 * z + 1)], axis=0)
+            scale = lax.rsqrt((st_all[h, 2 * z] + st_all[h, 2 * z + 1]) / hidden + NORM_EPS)
+            col = jnp.concatenate([unpack_column(scale, 0), unpack_column(scale, 1)], axis=0)
             for y in range(2):
                 gain = gain_ref[pl.ds(y * half, half)].astype(f32).reshape(1, half)
                 h2[h, 16 * z:16 * z + 16, y * half:(y + 1) * half] = (ag1[h, 2 * z + y].astype(f32) * col * gain).astype(bf)
@@ -266,35 +270,37 @@
         ag2[h, my] = o
         send_ag(mo, ag2, h, send_sem.at[10], ag2_sem)
 
+    project(0)
     rs1_send(0)
+    project(1)
+    rs1_send(1)
+    project(2)
     loads[1].wait()
     rs1_finish(0)
-    rs1_send(1)
-    stat_send(0)
+    stat_gather(0)
+    rs1_finish(1)
+    rs1_send(2)
+    stat_gather(1)
     for ld in loads[2:4]:
         ld.wait()
     norm(0)
 
-    lag2 = 5
-
     def body(t, carry):
-        h_now, j_now = t // n_j, t % n_j
-
-        @pl.when((h_now + 1 < n_h) & (j_now == 1))
-        def _():
-            rs1_finish(h_now + 1)
-
-        @pl.when((h_now + 2 < n_h) & (j_now == 2))
-        def _():
-            rs1_send(h_now + 2)
-
-        @pl.when((h_now + 1 < n_h) & (j_now == 4))
-        def _():
-            stat_send(h_now + 1)
-
-        @pl.when((t < steps) & (j_now == 0) & (t > 0))
-        def _():
-            norm(h_now)
+        @pl.when(t == n_j)
+        def _():
+            norm(1)
+
+        @pl.when(t == 2 * n_j)
+        def _():
+            norm(2)
+
+        @pl.when(t == n_j + 1)
+        def _():
+            rs1_finish(2)
+
+        @pl.when(t == n_j + 4)
+        def _():
+            stat_gather(2)
 
         @pl.when(t < steps)
         def _():
@@ -325,6 +331,8 @@
             def _():
                 rs2_send(s // n_j)
 
+        lag2 = LAG_RS
+
         @pl.when((t >= LAG_E + n_j - 1 + lag2) & ((t - LAG_E - (n_j - 1) - lag2) % n_j == 0))
         def _():
             rs2_finish((t - LAG_E - (n_j - 1) - lag2) // n_j)
@@ -333,17 +341,17 @@
 
     total_t = steps + LAG_E
     lax.fori_loop(0, total_t, body, 0)
-    done = len([h for h in range(n_h) if LAG_E + n_j - 1 + lag2 + h * n_j < total_t])
+    done = len([h for h in range(n_h) if LAG_E + n_j - 1 + LAG_RS + h * n_j < total_t])
     for h in range(done, n_h):
         rs2_finish(h)
     for h in range(n_h):
         wait_ag(ag2, h, send_sem.at[10], ag2_sem)
         for z in range(4):
             for y in range(2):
-                r0 = h * ROWS + z * 16
+                r0 = z * brows + h * 16
                 out_ref[r0:r0 + 16, y * half:(y + 1) * half] = ag2[h, 2 * z + y]
-    for k, ref in ((1, rs1), (2, rs1), (3, st_in.at[:, pl.ds(0, 3)]), (4, dr), (5, xs), (6, act.at[:, 0]), (7, act.at[:, 0]), (8, act.at[:, 0]), (9, rs2), (10, rs2)):
-        rcopy(ref, ref, send_sem.at[k], at_sem, core_dev).wait_send()
+    for k, ref in ((0, attn_v.at[:, pl.ds(0, 48)]), (11, st_all.at[:, pl.ds(0, 7)]), (1, rs1), (2, rs1), (3, st_in.at[:, pl.ds(0, 3)]), (4, dr), (5, xs), (6, act.at[:, 0]), (7, act.at[:, 0]), (8, act.at[:, 0]), (9, rs2), (10, rs2)):
+        rcopy(ref, ref, send_sem.at[k], at_sem.at[0], core_dev).wait_send()
 
 
 def mlp_call(x_in, gain, attn, w_o, w_gate, w_up, w_down, hidden):
@@ -364,21 +372,21 @@
         out_specs=vmem,
         scratch_shapes=[
             pltpu.VMEM((rows, cols), bf), pltpu.VMEM(w_o.shape, bf), pltpu.VMEM((n_j * CHUNK, cols), bf), pltpu.VMEM((n_j * CHUNK, cols), bf),
-            pltpu.VMEM((n_j * CHUNK, cols), bf), pltpu.VMEM((rows, attn.shape[1]), bf),
+            pltpu.VMEM((n_j * CHUNK, cols), bf), pltpu.VMEM((n_h, 64, attn.shape[1]), bf),
             pltpu.VMEM((n_h, 8, 16, half), bf), pltpu.VMEM((n_h, 7, 16, half), bf), pltpu.VMEM((n_h, 16, half), bf), pltpu.VMEM((n_h, 8, 16, half), bf),
-            pltpu.VMEM((n_h, 8, 128), f32), pltpu.VMEM((n_h, 4, 8, 128), f32), pltpu.VMEM((n_h, ROWS, cols), bf),
+            pltpu.VMEM((n_h, 8, 128), f32), pltpu.VMEM((n_h, 4, 8, 128), f32), pltpu.VMEM((n_h, 8, 128), f32), pltpu.VMEM((n_h, 8, 8, 128), f32), pltpu.VMEM((n_h, ROWS, cols), bf),
             pltpu.VMEM((steps, 2, 2, 16, 2 * CHUNK), bf), pltpu.VMEM((steps, 2, 16, 2 * CHUNK), bf), pltpu.VMEM((steps, 16, 2 * CHUNK), f32),
             pltpu.VMEM((steps, 16, 2 * CHUNK), bf), pltpu.VMEM((steps, 16, 2 * CHUNK), bf), pltpu.VMEM((steps, 4, 16, CHUNK), bf),
             pltpu.VMEM((n_h, ROWS, cols), f32),
             pltpu.VMEM((n_h, 8, 16, half), bf), pltpu.VMEM((n_h, 7, 16, half), bf), pltpu.VMEM((n_h, 16, half), bf), pltpu.VMEM((n_h, 8, 16, half), bf),
-            dma((5,)), dma((11,)), dma, dma((n_h,)), dma((n_h,)), dma((n_h,)), dma((n_h,)), dma((n_h,)),
+            dma((5,)), dma((12,)), dma((n_h,)), dma((n_h,)), dma((n_h,)), dma((n_h,)), dma((n_h,)), dma((n_h,)), dma((n_h,)),
             dma((steps,)), dma((steps,)), dma((steps,)), dma((steps,)), dma((steps,)),
         ],
         compiler_params=pltpu.CompilerParams(collective_id=1, has_side_effects=True, vmem_limit_bytes=VMEM_LIMIT),
     )(x_in, gain, attn, w_o, w_gate, w_up, w_down)
 
 
-GROUP_ROWS = 8
+GROUP_ROWS = 16
 
 
 def attn_kernel(seq_ref, proj_ref, bq_ref, bk_ref, bv_ref, freq_ref, k_hbm, v_hbm, attn_ref, ko_hbm, vo_hbm, kc, vc, qs, kn, vn, os, pos, in_sem, out_sem):

time: 106 us -> 100 us (0.943)
  Pallas kernels: 104 us -> 97.6 us
    pallas_call x1, Pallas kernels: 81.4 us -> 75.8 us  [mlp_call(): pl.pallas_call(functools.partial(mlp_kernel, hidden), name='mlp', out_sha...]
where the time goes in v3:
time: 100 us
  Pallas kernels  97.6 us (98%)
  local copies, waits for them, and re-layouts  1.84 us (2%)
    pallas_call x1, Pallas kernels, mlp_call(): pl.pallas_call(functools.partial(mlp_kernel, hidden), name='mlp', out_sha...  75.8 us
    pallas_call x1, Pallas kernels, qkv_call(): pl.pallas_call(functools.partial(qkv_kernel, hidden), name='qkv', out_sha...  13.4 us
    pallas_call x1, Pallas kernels, attn_call(): pl.pallas_call(attn_kernel, name='attn', out_shape=(jax.ShapeDtypeStruct(...  8.44 us

profile of v3, /device:TPU:0, one launch (start us, length us, event | category | flops | bytes accessed | tf_op | source)
XLA Modules:
  0.0 100.1 jit_solution(4092810399215962572)
XLA Ops:
  0.6 13.4 %qkv.1.proj_ref = f32[48,896]{1,0:T(8,128)} custom-call(bf16[192,1280]{1,0:T(8,128)(2,1)} %x_hbm.3, bf16[1280]{0:T(1024)(128)(2,1)} %gain_ref.2, bf16[1280,640]{1,0:T(8,128)(2,1)} %wq_hbm.1, bf16[1280,128]{1,0:T(8,128)(2,1)} %wk_hbm.1, bf16[1280,128]{1,0:T(8,128)(2,1)} %wv_hbm.1), custom_call_target="tpu_custom_call" | custom-call | tf_op jit(solution)/shard_map/qkv/pallas_call | solution.py:103
  14.0 8.4 %attn.1 = (bf16[48,640]{1,0:T(8,128)(2,1)}, bf16[48,384,128]{2,1,0:T(8,128)(2,1)}, bf16[48,384,128]{2,1,0:T(8,128)(2,1)}) custom-call(s32[48]{0:T(128)} %seq_ref.1, f32[48,896]{1,0:T(8,128)} %qkv.1.proj_ref, bf16[640]{0:T(1024)(128)(2,1)} %bq_ref.1, bf16[128]{0:T(256)(128)(2,1)} %bk_ref.1, bf16[128]{0:T(256)(128)(2,1)} %bv_ref.1, ...), custom_call_target="tpu_custom_call" | custom-call | tf_op jit(solution)/shard_map/attn/pallas_call | solution.py:471
  22.5 75.8 %mlp.1 = bf16[192,1280]{1,0:T(8,128)(2,1)} custom-call(bf16[192,1280]{1,0:T(8,128)(2,1)} %x_hbm.3, bf16[1280]{0:T(1024)(128)(2,1)} %gain_ref.3, bf16[48,640]{1,0:T(8,128)(2,1)} %get-tuple-element.6.attn_ref, bf16[640,1280]{1,0:T(8,128)(2,1)} %wo_hbm.1, bf16[3424,1280]{1,0:T(8,128)(2,1)} %bitcast.10, bf16[3424,1280]{1,0:T(8,128)(2,1)} %bitcast.11, ...), custom_call_target="tpu_custom_call" | custom-call | tf_op jit(solution)/shard_map/mlp/pallas_call | solution.py:367
  98.2 1.8 %copy.23 = bf16[192,1280]{1,0:T(8,128)(2,1)} copy(bf16[192,1280]{1,0:T(8,128)(2,1)} %mlp.1) | data formatting | bytes 983040

commit v4 on v3

--- a/solution.py
+++ b/solution.py
@@ -13,9 +13,11 @@
 ROPE_THETA = 1000000.0
 MESH = pl.DeviceIdType.MESH
 CHUNK = 512
+TILE = 256
 ROWS = 64
 LAG_B, LAG_C, LAG_D, LAG_E, LAG_RS = 1, 4, 7, 8, 8
-VMEM_LIMIT = 66 * 1024 * 1000
+VMEM_LIMIT = 67043328
+MLP_LIMIT = VMEM_LIMIT
 
 
 def rcopy(src, dst, send_sem, recv_sem, dev):
@@ -117,9 +119,9 @@
     )(x_in, gain, w_q, w_k, w_v)
 
 
-def mlp_kernel(hidden, x_hbm, gain_ref, attn_ref, wo_hbm, wg_hbm, wu_hbm, wd_hbm, out_ref,
+def mlp_kernel(hidden, x_hbm, gain_ref, attn_ref, wo_hbm, wg_hbm, wu_hbm, wd_hbm, ag2,
                x_v, wo_v, wg_v, wu_v, wd_v, attn_v, p1, rs1, mp, ag1, st_own, st_in, st_sum, st_all, h2,
-               pp, dr, own, xs, xr, act, dacc, p2, rs2, mo, ag2,
+               pp, dr, own, xs, xr, act, dacc, p2, rs2, mo, eye,
                ld_sem, send_sem, at_sem, rs1_sem, ag1_sem, st_sem, sg_sem, rs2_sem, ag2_sem, d_sem, x_sem, ax_sem, ad_sem, af_sem):
     my, mx = lax.axis_index("my"), lax.axis_index("mx")
     n_my = 8
@@ -135,8 +137,10 @@
     brows = attn_ref.shape[0]
     f32, bf = jnp.float32, jnp.bfloat16
 
+    n_k = wg_v.shape[0]
+    tiles = [(src.at[:, pl.ds(TILE * k, TILE)], dst.at[k, pl.ds(0, ff)]) for src, dst in ((wg_hbm, wg_v), (wu_hbm, wu_v)) for k in range(n_k)]
     loads = [pltpu.make_async_copy(s, d, ld_sem.at[i]) for i, (s, d) in enumerate([
-        (wo_hbm, wo_v), (x_hbm, x_v), (wg_hbm, wg_v.at[pl.ds(0, ff)]), (wu_hbm, wu_v.at[pl.ds(0, ff)]), (wd_hbm, wd_v.at[pl.ds(0, ff)])])]
+        (wo_hbm, wo_v), (x_hbm, x_v)] + tiles + [(wd_hbm, wd_v.at[pl.ds(0, ff)])])]
     for ld in loads:
         ld.start()
     barrier = pltpu.get_barrier_semaphore()
@@ -153,8 +157,11 @@
     for h in range(n_h):
         attn_v[h, mine, :] = attn_ref[16 * h:16 * h + 16, :]
     dacc[...] = jnp.zeros_like(dacc)
-    for w in (wg_v, wu_v, wd_v):
-        w[ff:, :] = jnp.zeros((w.shape[0] - ff, w.shape[1]), bf)
+    wd_v[ff:, :] = jnp.zeros((wd_v.shape[0] - ff, wd_v.shape[1]), bf)
+    for w in (wg_v, wu_v):
+        for k in range(n_k):
+            w[k, ff:, :] = jnp.zeros((w.shape[1] - ff, TILE), bf)
+    eye[...] = (lax.broadcasted_iota(jnp.int32, (TILE, TILE), 0) == lax.broadcasted_iota(jnp.int32, (TILE, TILE), 1)).astype(f32).astype(bf)
     loads[0].wait()
 
     zs = (3 - zi, (zi + 2) % 4, zi + 1 - 2 * (zi % 2), zi)
@@ -168,37 +175,51 @@
             for z in range(4):
                 p1[h, 2 * z + y] = r[16 * z:16 * z + 16]
 
+    parts = ((0, TILE), (TILE, half))
+
     def send_rs(p, rs, h, ssem, rsem):
-        for k, peer in enumerate(peers):
-            rcopy(p.at[h, peer], rs.at[h, k], ssem, rsem.at[h], {"my": peer}).start()
-
-    def finish_rs(p, rs, h, ssem, rsem, base):
-        rcopy(rs.at[h], rs.at[h], ssem, rsem.at[h], {"my": my}).wait_recv()
-        total = p[h, my].astype(f32)
-        for i in range(n_my - 1):
-            total += rs[h, i].astype(f32)
+        for i, (lo, hi) in enumerate(parts):
+            cols = pl.ds(lo, hi - lo)
+            for k, peer in enumerate(peers):
+                rcopy(p.at[h, peer, :, cols], rs.at[h, k, :, cols], ssem, rsem.at[h, i], {"my": peer}).start()
+
+    def finish_rs(p, rs, h, i, ssem, rsem, base):
+        lo, hi = parts[i]
+        seven = rs.at[h, :, :, pl.ds(lo, hi - lo)]
+        rcopy(seven, seven, ssem, rsem.at[h, i], {"my": my}).wait_recv()
+        total = p[h, my, :, lo:hi].astype(f32)
+        for k in range(n_my - 1):
+            total += rs[h, k, :, lo:hi].astype(f32)
         return (base + total).astype(bf)
 
-    def send_ag(piece, ag, h, ssem, rsem):
+    def send_ag(piece, ag, h, ssem, rsem, i=None):
+        src, dst, sem = piece.at[h], ag.at[h, my], rsem.at[h]
+        if i is not None:
+            cols = pl.ds(parts[i][0], parts[i][1] - parts[i][0])
+            src, dst, sem = piece.at[h, :, cols], ag.at[h, my, :, cols], rsem.at[h, i]
         for peer in peers:
-            rcopy(piece.at[h], ag.at[h, my], ssem, rsem.at[h], {"my": peer}).start()
-
-    def wait_ag(ag, h, ssem, rsem):
-        seven = ag.at[h, pl.ds(0, n_my - 1)]
-        rcopy(seven, seven, ssem, rsem.at[h], {"my": my}).wait_recv()
+            rcopy(src, dst, ssem, sem, {"my": peer}).start()
+
+    def wait_ag(ag, h, ssem, rsem, i=None):
+        seven, sem = ag.at[h, pl.ds(0, n_my - 1)], rsem.at[h] if i is None else rsem.at[h, i]
+        if i is not None:
+            seven = ag.at[h, pl.ds(0, n_my - 1), :, pl.ds(parts[i][0], parts[i][1] - parts[i][0])]
+        rcopy(seven, seven, ssem, sem, {"my": my}).wait_recv()
 
     def rs1_send(h):
         send_rs(p1, rs1, h, send_sem.at[1], rs1_sem)
 
     def rs1_finish(h):
-        r0 = pl.multiple_of(zi * brows + h * 16, 16)
-        base = x_v[pl.ds(r0, 16), pl.ds(pl.multiple_of(yi * half, 128), half)].astype(f32)
-        m = finish_rs(p1, rs1, h, send_sem.at[1], rs1_sem, base)
-        mp[h] = m
-        ag1[h, my] = m
-        send_ag(mp, ag1, h, send_sem.at[2], ag1_sem)
-        m = m.astype(f32)
-        ss = jnp.sum(m * m, axis=1, keepdims=True)
+        ss = jnp.zeros((16, 1), f32)
+        for i, (lo, hi) in enumerate(parts):
+            r0 = pl.multiple_of(zi * brows + h * 16, 16)
+            base = x_v[pl.ds(r0, 16), pl.ds(pl.multiple_of(yi * half + lo, 128), hi - lo)].astype(f32)
+            m = finish_rs(p1, rs1, h, i, send_sem.at[1], rs1_sem, base)
+            mp[h, :, lo:hi] = m
+            ag1[h, my, :, lo:hi] = m
+            send_ag(mp, ag1, h, send_sem.at[2], ag1_sem, i)
+            m = m.astype(f32)
+            ss += jnp.sum(m * m, axis=1, keepdims=True)
         tile = pack_column([ss[:8], ss[8:]])
         st_own[h] = tile
         st_in[h, mx] = tile
@@ -215,7 +236,8 @@
 
     def norm(h):
         wait_ag(st_all, h, send_sem.at[11], sg_sem)
-        wait_ag(ag1, h, send_sem.at[2], ag1_sem)
+        for i in range(2):
+            wait_ag(ag1, h, send_sem.at[2], ag1_sem, i)
         for z in range(4):
             scale = lax.rsqrt((st_all[h, 2 * z] + st_all[h, 2 * z + 1]) / hidden + NORM_EPS)
             col = jnp.concatenate([unpack_column(scale, 0), unpack_column(scale, 1)], axis=0)
@@ -223,12 +245,26 @@
                 gain = gain_ref[pl.ds(y * half, half)].astype(f32).reshape(1, half)
                 h2[h, 16 * z:16 * z + 16, y * half:(y + 1) * half] = (ag1[h, 2 * z + y].astype(f32) * col * gain).astype(bf)
 
+    def transpose(i, carry):
+        rows = pl.ds(pl.multiple_of(i * TILE, TILE), TILE)
+        for k in range(n_k):
+            flipped = [lax.dot_general(eye[...], w[k, rows, :], (((1,), (1,)), ((), ())), preferred_element_type=f32).astype(bf) for w in (wg_v, wu_v)]
+            for w, val in zip((wg_v, wu_v), flipped):
+                w[k, rows, :] = val
+        return carry
+
     def stage_a(s):
         h, j = s // n_j, s % n_j
         lhs = h2[h]
-        part_rows = pl.ds(pl.multiple_of(j * CHUNK, CHUNK), CHUNK)
         for i, w in enumerate((wg_v, wu_v)):
-            val = lax.dot_general(lhs, w[part_rows, :], (((1,), (1,)), ((), ())), preferred_element_type=f32).astype(bf)
+            cols = []
+            for n in range(CHUNK // TILE):
+                rows = pl.ds(pl.multiple_of(j * CHUNK + n * TILE, TILE), TILE)
+                acc = jnp.dot(lhs[:, :TILE], w[0, rows, :], preferred_element_type=f32)
+                for k in range(1, n_k):
+                    acc += jnp.dot(lhs[:, TILE * k:TILE * (k + 1)], w[k, rows, :], preferred_element_type=f32)
+                cols.append(acc.astype(bf))
+            val = jnp.concatenate(cols, axis=1)
             for m in range(4):
                 pp[s, m % 2, m // 2, :, i * CHUNK:(i + 1) * CHUNK] = val[16 * m:16 * m + 16]
         rcopy(pp.at[s, 1 - ci], dr.at[s], send_sem.at[4], d_sem.at[s], core_dev).start()
@@ -265,24 +301,29 @@
         send_rs(p2, rs2, h, send_sem.at[9], rs2_sem)
 
     def rs2_finish(h):
-        o = finish_rs(p2, rs2, h, send_sem.at[9], rs2_sem, mp[h].astype(f32))
-        mo[h] = o
-        ag2[h, my] = o
-        send_ag(mo, ag2, h, send_sem.at[10], ag2_sem)
-
+        for i, (lo, hi) in enumerate(parts):
+            o = finish_rs(p2, rs2, h, i, send_sem.at[9], rs2_sem, mp[h, :, lo:hi].astype(f32))
+            mo[h, :, lo:hi] = o
+            ag2[h, my, :, lo:hi] = o
+            send_ag(mo, ag2, h, send_sem.at[10], ag2_sem, i)
+
+    n_t = n_j * (CHUNK // TILE)
     project(0)
     rs1_send(0)
     project(1)
     rs1_send(1)
     project(2)
     loads[1].wait()
+    for ld in loads[2:2 + 2 * n_k]:
+        ld.wait()
+    lax.fori_loop(0, n_t // 2, transpose, 0)
     rs1_finish(0)
+    lax.fori_loop(n_t // 2, n_t // 2 + 3, transpose, 0)
     stat_gather(0)
     rs1_finish(1)
     rs1_send(2)
+    lax.fori_loop(n_t // 2 + 3, n_t, transpose, 0)
     stat_gather(1)
-    for ld in loads[2:4]:
-        ld.wait()
     norm(0)
 
     def body(t, carry):
@@ -320,7 +361,7 @@
 
         @pl.when(t == LAG_E)
         def _():
-            loads[4].wait()
+            loads[-1].wait()
 
         @pl.when(t >= LAG_E)
         def _():
@@ -345,11 +386,8 @@
     for h in range(done, n_h):
         rs2_finish(h)
     for h in range(n_h):
-        wait_ag(ag2, h, send_sem.at[10], ag2_sem)
-        for z in range(4):
-            for y in range(2):
-                r0 = z * brows + h * 16
-                out_ref[r0:r0 + 16, y * half:(y + 1) * half] = ag2[h, 2 * z + y]
+        for i in range(2):
+            wait_ag(ag2, h, send_sem.at[10], ag2_sem, i)
     for k, ref in ((0, attn_v.at[:, pl.ds(0, 48)]), (11, st_all.at[:, pl.ds(0, 7)]), (1, rs1), (2, rs1), (3, st_in.at[:, pl.ds(0, 3)]), (4, dr), (5, xs), (6, act.at[:, 0]), (7, act.at[:, 0]), (8, act.at[:, 0]), (9, rs2), (10, rs2)):
         rcopy(ref, ref, send_sem.at[k], at_sem.at[0], core_dev).wait_send()
 
@@ -362,28 +400,42 @@
     steps = n_h * n_j
     half = cols // 2
     bf, f32 = jnp.bfloat16, jnp.float32
-    any_spec, vmem = pl.BlockSpec(memory_space=pl.ANY), pl.BlockSpec(memory_space=pltpu.VMEM)
+    hbm, vmem = pl.BlockSpec(memory_space=pltpu.HBM), pl.BlockSpec(memory_space=pltpu.VMEM)
     dma = pltpu.SemaphoreType.DMA
     return pl.pallas_call(
         functools.partial(mlp_kernel, hidden),
         name="mlp",
-        out_shape=jax.ShapeDtypeStruct((rows, cols), bf),
-        in_specs=[any_spec, vmem, vmem, any_spec, any_spec, any_spec, any_spec],
+        out_shape=jax.ShapeDtypeStruct((n_h, 8, 16, half), bf),
+        in_specs=[hbm, vmem, vmem, hbm, hbm, hbm, hbm],
         out_specs=vmem,
         scratch_shapes=[
-            pltpu.VMEM((rows, cols), bf), pltpu.VMEM(w_o.shape, bf), pltpu.VMEM((n_j * CHUNK, cols), bf), pltpu.VMEM((n_j * CHUNK, cols), bf),
+            pltpu.VMEM((rows, cols), bf), pltpu.VMEM(w_o.shape, bf), pltpu.VMEM((cols // TILE, n_j * CHUNK, TILE), bf), pltpu.VMEM((cols // TILE, n_j * CHUNK, TILE), bf),
             pltpu.VMEM((n_j * CHUNK, cols), bf), pltpu.VMEM((n_h, 64, attn.shape[1]), bf),
             pltpu.VMEM((n_h, 8, 16, half), bf), pltpu.VMEM((n_h, 7, 16, half), bf), pltpu.VMEM((n_h, 16, half), bf), pltpu.VMEM((n_h, 8, 16, half), bf),
             pltpu.VMEM((n_h, 8, 128), f32), pltpu.VMEM((n_h, 4, 8, 128), f32), pltpu.VMEM((n_h, 8, 128), f32), pltpu.VMEM((n_h, 8, 8, 128), f32), pltpu.VMEM((n_h, ROWS, cols), bf),
             pltpu.VMEM((steps, 2, 2, 16, 2 * CHUNK), bf), pltpu.VMEM((steps, 2, 16, 2 * CHUNK), bf), pltpu.VMEM((steps, 16, 2 * CHUNK), f32),
             pltpu.VMEM((steps, 16, 2 * CHUNK), bf), pltpu.VMEM((steps, 16, 2 * CHUNK), bf), pltpu.VMEM((steps, 4, 16, CHUNK), bf),
             pltpu.VMEM((n_h, ROWS, cols), f32),
-            pltpu.VMEM((n_h, 8, 16, half), bf), pltpu.VMEM((n_h, 7, 16, half), bf), pltpu.VMEM((n_h, 16, half), bf), pltpu.VMEM((n_h, 8, 16, half), bf),
-            dma((5,)), dma((12,)), dma((n_h,)), dma((n_h,)), dma((n_h,)), dma((n_h,)), dma((n_h,)), dma((n_h,)), dma((n_h,)),
+            pltpu.VMEM((n_h, 8, 16, half), bf), pltpu.VMEM((n_h, 7, 16, half), bf), pltpu.VMEM((n_h, 16, half), bf), pltpu.VMEM((TILE, TILE), bf),
+            dma((3 + 2 * (cols // TILE),)), dma((12,)), dma((n_h,)), dma((n_h, 2)), dma((n_h, 2)), dma((n_h,)), dma((n_h,)), dma((n_h, 2)), dma((n_h, 2)),
             dma((steps,)), dma((steps,)), dma((steps,)), dma((steps,)), dma((steps,)),
         ],
-        compiler_params=pltpu.CompilerParams(collective_id=1, has_side_effects=True, vmem_limit_bytes=VMEM_LIMIT),
+        compiler_params=pltpu.CompilerParams(collective_id=1, has_side_effects=True, vmem_limit_bytes=MLP_LIMIT),
     )(x_in, gain, attn, w_o, w_gate, w_up, w_down)
+
+
+def place_kernel(pieces_ref, out_ref):
+    n_h, _, _, half = pieces_ref.shape
+    for h in range(n_h):
+        for z in range(4):
+            for y in range(2):
+                r0 = z * 16 * n_h + h * 16
+                out_ref[r0:r0 + 16, y * half:(y + 1) * half] = pieces_ref[h, 2 * z + y]
+
+
+def place_call(pieces, shape):
+    vmem = pl.BlockSpec(memory_space=pltpu.VMEM)
+    return pl.pallas_call(place_kernel, name="place", out_shape=jax.ShapeDtypeStruct(shape, pieces.dtype), in_specs=[vmem], out_specs=vmem, compiler_params=pltpu.CompilerParams(vmem_limit_bytes=4 * 1024 * 1024))(pieces)
 
 
 GROUP_ROWS = 16
@@ -494,7 +546,8 @@
         hidden = x_in.shape[1] * mx_size
         projected = qkv_call(x_in, gain_attn, w_q, w_k, w_v, hidden)
         attn_rows, k_out, v_out = attn_call(seq_lens, projected, b_q, b_k, b_v, k_cache, v_cache)
-        x_out = mlp_call(x_in, gain_mlp, attn_rows, w_o, w_gate.T, w_up.T, w_down, hidden)
+        pieces = mlp_call(x_in, gain_mlp, attn_rows, w_o, w_gate.T, w_up.T, w_down, hidden)
+        x_out = place_call(pieces, x_in.shape)
         k_cache_out, v_cache_out = k_out.reshape(k_cache.shape), v_out.reshape(v_cache.shape)
         return x_out, k_cache_out, v_cache_out
 

time: 100 us -> 96 us (0.960)
  Pallas kernels: 97.6 us -> 94.1 us
    pallas_call x1, Pallas kernels: 75.8 us -> 71.5 us  [mlp_call(): pl.pallas_call(functools.partial(mlp_kernel, hidden), name='mlp', out_sha...]
where the time goes in v4:
time: 96 us; the launch traced here: 95.8 us
  Pallas kernels  94.1 us (98%)
  local copies, waits for them, and re-layouts  1.02 us (1%)
    pallas_call x1, Pallas kernels, mlp_call(): pl.pallas_call(functools.partial(mlp_kernel, hidden), name='mlp', out_sha...  71.5 us
    pallas_call x1, Pallas kernels, qkv_call(): pl.pallas_call(functools.partial(qkv_kernel, hidden), name='qkv', out_sha...  13.4 us
    pallas_call x1, Pallas kernels, attn_call(): pl.pallas_call(attn_kernel, name='attn', out_shape=(jax.ShapeDtypeStruct(...  8.44 us

profile of v4, /device:TPU:0, one launch (start us, length us, event | category | flops | bytes accessed | tf_op | source)
XLA Modules:
  0.0 95.8 jit_solution(11052731706295366845)
XLA Ops:
  0.6 13.4 %qkv.1.proj_ref = f32[48,896]{1,0:T(8,128)} custom-call(bf16[192,1280]{1,0:T(8,128)(2,1)} %x_hbm.3, bf16[1280]{0:T(1024)(128)(2,1)} %gain_ref.2, bf16[1280,640]{1,0:T(8,128)(2,1)} %wq_hbm.1, bf16[1280,128]{1,0:T(8,128)(2,1)} %wk_hbm.1, bf16[1280,128]{1,0:T(8,128)(2,1)} %wv_hbm.1), custom_call_target="tpu_custom_call" | custom-call | tf_op jit(solution)/shard_map/qkv/pallas_call | solution.py:105
  14.0 8.4 %attn.1 = (bf16[48,640]{1,0:T(8,128)(2,1)}, bf16[48,384,128]{2,1,0:T(8,128)(2,1)}, bf16[48,384,128]{2,1,0:T(8,128)(2,1)}) custom-call(s32[48]{0:T(128)} %seq_ref.1, f32[48,896]{1,0:T(8,128)} %qkv.1.proj_ref, bf16[640]{0:T(1024)(128)(2,1)} %bq_ref.1, bf16[128]{0:T(256)(128)(2,1)} %bk_ref.1, bf16[128]{0:T(256)(128)(2,1)} %bv_ref.1, ...), custom_call_target="tpu_custom_call" | custom-call | tf_op jit(solution)/shard_map/attn/pallas_call | solution.py:523
  22.4 71.5 %mlp.1.pieces_ref = bf16[3,8,16,640]{3,2,1,0:T(8,128)(2,1)} custom-call(bf16[192,1280]{1,0:T(8,128)(2,1)} %x_hbm.3, bf16[1280]{0:T(1024)(128)(2,1)} %gain_ref.3, bf16[48,640]{1,0:T(8,128)(2,1)} %get-tuple-element.6.attn_ref, bf16[640,1280]{1,0:T(8,128)(2,1)} %wo_hbm.1, bf16[3424,1280]{1,0:T(8,128)(2,1)} %bitcast.10, bf16[3424,1280]{1,0:T(8,128)(2,1)} %bitcast.11, ...), custom_call_target="tpu_custom_call" | custom-call | tf_op jit(solution)/shard_map/mlp/pallas_call | solution.py:405
  94.0 0.0 copy-start
  94.0 1.0 %copy-done = bf16[3,8,16,640]{3,2,1,0:T(8,128)(2,1)S(1)} copy-done((bf16[3,8,16,640]{3,2,1,0:T(8,128)(2,1)S(1)}, bf16[3,8,16,640]{3,2,1,0:T(8,128)(2,1)}, u32[]{:S(2)}) %copy-start) | copy-done | bytes 491544
  95.0 0.8 place.1
Async XLA Ops:
  94.0 1.0 %copy-start = (bf16[3,8,16,640]{3,2,1,0:T(8,128)(2,1)S(1)}, bf16[3,8,16,640]{3,2,1,0:T(8,128)(2,1)}, u32[]{:S(2)}) copy-start(bf16[3,8,16,640]{3,2,1,0:T(8,128)(2,1)} %mlp.1.pieces_ref) | copy-start | bytes 1474564
